TPU v7x, 32 devices: a whole 2x2x4 slice. The times are simulated.
32 devices in a mesh: dp: 2 (over x), tp: 4 (over z), sp: 4 (over y, core).
Axes of the slice: x: 2, y: 2, z: 4, core: 2. Of those that a mesh axis runs over, the one named last changes fastest.
Arguments:
- hidden: bfloat16 [32, 4096], P('dp'), parts along dimension 0
- positions: int32 [32], P('dp'), parts along dimension 0
- norm_attn: float32 [4096], replicated
- norm_mlp: float32 [4096], replicated
- w_qkv: bfloat16 [4096, 6144], P(None, 'tp')
- w_out: bfloat16 [4096, 4096], P('tp')
- w_gate_up: bfloat16 [4096, 28672], P(None, 'tp')
- w_down: bfloat16 [14336, 4096], P('tp')
- k_cache: bfloat16 [32, 4096, 8, 128], P('dp', 'sp', 'tp'), parts along dimension 0
- v_cache: bfloat16 [32, 4096, 8, 128], P('dp', 'sp', 'tp'), parts along dimension 0
Outputs:
- output 1: bfloat16 [32, 4096], P('dp'), parts along dimension 0
- output 2: bfloat16 [32, 4096, 8, 128], P('dp', 'sp', 'tp'), parts along dimension 0
- output 3: bfloat16 [32, 4096, 8, 128], P('dp', 'sp', 'tp'), parts along dimension 0
There are 2 independent parts. A program takes and returns all parts, laid end to end along the dimension named above; an argument that names none is the same for every part.
All inputs are finite; a program needn't handle non-finite values.
Results may differ from a plain program's by a relative error of at most 0.00869568.
Values sent between devices are 32-bit elements.
A program may use at most 1 GiB of HBM per device.

v0:
```python
import jax
import jax.numpy as jnp
from jax import lax
from jax.sharding import PartitionSpec as P

WINDOW = 2047
ROPE_BASE = 10000.0
NORM_EPS = 1e-5


def rms_norm(values, gain_vec):
    mean_sq = jnp.mean(values * values, axis=-1, keepdims=True)
    return values * lax.rsqrt(mean_sq + NORM_EPS) * gain_vec


def rope_tables(positions, head_dim):
    inv_freq = ROPE_BASE ** (-jnp.arange(0, head_dim, 2).astype(jnp.float32) / head_dim)
    angles = positions.astype(jnp.float32)[:, None] * inv_freq[None, :]
    angles = jnp.concatenate([angles, angles], axis=-1)
    return jnp.cos(angles), jnp.sin(angles)


def rotate_half(values, cos_tab, sin_tab):
    half_dim = values.shape[-1] // 2
    turned = jnp.concatenate([-values[..., half_dim:], values[..., :half_dim]], axis=-1)
    return values * cos_tab + turned * sin_tab


def new_entries(hidden, positions, norm_attn, w_qkv, kv_count, head_dim):
    num_rows = hidden.shape[0]
    resid_in = hidden.astype(jnp.float32)
    normed = rms_norm(resid_in, norm_attn).astype(jnp.bfloat16)
    group_size = w_qkv.shape[1] // (kv_count * head_dim) - 2
    qkv_proj = jnp.dot(normed, w_qkv, preferred_element_type=jnp.float32).reshape(num_rows, kv_count, group_size + 2, head_dim)
    cos_tab, sin_tab = rope_tables(positions, head_dim)
    q_new = rotate_half(qkv_proj[:, :, :group_size], cos_tab[:, None, None], sin_tab[:, None, None]).astype(jnp.bfloat16)
    k_new = rotate_half(qkv_proj[:, :, group_size], cos_tab[:, None], sin_tab[:, None]).astype(jnp.bfloat16)
    v_new = qkv_proj[:, :, group_size + 1].astype(jnp.bfloat16)
    return resid_in, q_new, k_new, v_new


def write_entry(cache, entry, slot_ids, positions):
    at_slot = (slot_ids[None, :] == positions[:, None])[:, :, None, None]
    return jnp.where(at_slot, entry[:, None], cache)


def window_attention(q_new, k_block, v_block, slot_ids, positions):
    score_scale = q_new.shape[-1] ** -0.5
    scores = jnp.einsum('bkgd,bjkd->bkgj', q_new, k_block, preferred_element_type=jnp.float32) * score_scale
    in_window = (slot_ids[None, :] <= positions[:, None]) & (slot_ids[None, :] >= positions[:, None] - WINDOW)
    scores = jnp.where(in_window[:, None, None, :], scores, -jnp.inf)
    glob_max = lax.pmax(jnp.max(scores, axis=-1), 'sp')
    weights = jnp.exp(scores - glob_max[..., None])
    weight_sum = lax.psum(jnp.sum(weights, axis=-1), 'sp')
    acc_sum = lax.psum(jnp.einsum('bkgj,bjkd->bkgd', weights.astype(jnp.bfloat16), v_block, preferred_element_type=jnp.float32), 'sp')
    return (acc_sum / weight_sum[..., None]).astype(jnp.bfloat16)


def layer_tail(resid_in, attended, norm_mlp, w_out, w_gate_up, w_down):
    out_part = jnp.dot(attended, w_out, preferred_element_type=jnp.float32).astype(jnp.bfloat16).astype(jnp.float32)
    mid_resid = resid_in + lax.psum(out_part, 'tp')
    normed_mlp = rms_norm(mid_resid, norm_mlp).astype(jnp.bfloat16)
    gate_up = jnp.dot(normed_mlp, w_gate_up, preferred_element_type=jnp.float32)
    ffn_local = w_down.shape[0]
    act_vals = (jax.nn.silu(gate_up[:, :ffn_local]) * gate_up[:, ffn_local:]).astype(jnp.bfloat16)
    down_part = jnp.dot(act_vals, w_down, preferred_element_type=jnp.float32).astype(jnp.bfloat16).astype(jnp.float32)
    result = mid_resid + lax.psum(down_part, 'tp')
    return result.astype(jnp.bfloat16)


def solution(mesh):
    cache_spec = P('dp', 'sp', 'tp', None)

    def local_step(hidden, positions, norm_attn, norm_mlp, w_qkv, w_out, w_gate_up, w_down, k_cache, v_cache):
        num_rows, block_len, kv_local, head_dim = k_cache.shape
        resid_in, q_new, k_new, v_new = new_entries(hidden, positions, norm_attn, w_qkv, kv_local, head_dim)
        slot_ids = lax.axis_index('sp') * block_len + jnp.arange(block_len)
        k_upd = write_entry(k_cache, k_new, slot_ids, positions)
        v_upd = write_entry(v_cache, v_new, slot_ids, positions)
        attended = window_attention(q_new, k_upd, v_upd, slot_ids, positions).reshape(num_rows, -1)
        result = layer_tail(resid_in, attended, norm_mlp, w_out, w_gate_up, w_down)
        return result, k_upd, v_upd

    return jax.shard_map(local_step, mesh=mesh, in_specs=(P('dp', None), P('dp'), P(None), P(None), P(None, 'tp'), P('tp', None), P(None, 'tp'), P('tp', None), cache_spec, cache_spec), out_specs=(P('dp', None), cache_spec, cache_spec), check_vma=False)
```

profile of v0, /device:TPU:0, one launch (start us, length us, event | category | flops | bytes accessed | tf_op | source)
XLA Modules:
  0.0 217.0 jit_solution(15897038214842997809)
XLA Ops:
  7.2 1.1 fusion.14
  8.3 6.5 %fusion.21 = f32[16,1536]{1,0:T(8,128)S(1)} fusion(bf16[4096,1536]{1,0:T(8,128)(2,1)} %param.14, bf16[16,4096]{1,0:T(8,128)(2,1)} %param.10, f32[4096]{0:T(1024)} %param.12, f32[16]{0:T(128)S(1)} %add_rsqrt_fusion.1), kind=kOutput, calls=%fused_computation.28 | convolution fusion | flops 201588736 | bytes 12828736 | tf_op jit(solution)/shard_map/dot_general | solution.py:34
  14.8 0.1 slice_negate_fusion
  15.1 0.1 fusion.37
  15.2 0.1 slice_negate_fusion.1
  15.3 0.1 compare_and_fusion
  15.4 0.1 fusion.35
  15.5 26.2 %broadcast_select_fusion.1 = (bf16[16,1024,2,128]{3,2,1,0:T(2,128)(2,1)S(1)}, bf16[16,1024,2,128]{3,2,1,0:T(2,128)(2,1)}) fusion(bf16[16,1024,2,128]{3,2,1,0:T(2,128)(2,1)} %param.18, pred[16,1024]{1,0:T(8,128)(4,1)S(1)} %get-tuple-element.12, bf16[16,2,128]{2,1,0:T(2,128)(2,1)S(1)} %fusion.35, bf16[16,1024,2,128]{3,2,1,0:T(2,128)(2,1)} %param.19, ...), kind=kLoop, calls=%fused_computation.1 | loop fusion | flops 8388608 | bytes 33587200 | tf_op jit(solution)/shard_map/jit(_where)/select_n | solution.py:44
  41.7 3.4 %copy-done = bf16[16,1024,2,128]{3,2,1,0:T(2,128)(2,1)} copy-done((bf16[16,1024,2,128]{3,2,1,0:T(2,128)(2,1)}, bf16[16,1024,2,128]{3,2,1,0:T(2,128)(2,1)S(1)}, u32[]{:S(2)}) %copy-start) | copy-done | bytes 8388632
  45.1 2.4 %fusion.40 = (f32[16,2,4]{2,1,0:T(2,128)S(1)}, f32[16,2,4,1024]{3,2,1,0:T(4,128)S(1)}) fusion(bf16[16,1024,2,128]{3,2,1,0:T(2,128)(2,1)S(1)} %get-tuple-element.5, f32[16,2,6,128]{3,2,1,0:T(8,128)S(1)} %reshape.247, f32[16,2,4,64]{3,2,1,0:T(4,128)S(1)} %get-tuple-element.4, f32[16,2,4,64]{3,2,1,0:T(4,128)S(1)} %get-tuple-element.3, ...), kind=kOutput, calls=%fused_computation.61 | convolution fusion | flops 34029440 | bytes 9142784 | tf_op jit(solution)/shard_map/bkgd,bjkd->bkgj/dot_general | solution.py:49
  47.5 12.7 %pmax.7 = f32[16,2,4]{2,1,0:T(2,128)S(1)} all-reduce(f32[16,2,4]{2,1,0:T(2,128)S(1)} %get-tuple-element.15), channel_id=1, replica_groups=mesh['dp'=2,'tp'=4,'sp'=4] {'sp'}, use_global_device_ids=true, to_apply=%region_2.3 | all-reduce | flops 128 | bytes 1024 | tf_op jit(solution)/shard_map/pmax | solution.py:52
  60.2 5.4 %fusion = f32[16,2,4,128]{3,2,1,0:T(4,128)} fusion(bf16[16,1024,2,128]{3,2,1,0:T(2,128)(2,1)} %get-tuple-element.6, f32[16,2,4,1024]{3,2,1,0:T(4,128)S(1)} %get-tuple-element.16, f32[16,2,4]{2,1,0:T(2,128)S(1)} %pmax.7), kind=kOutput, calls=%fused_computation.2 | convolution fusion | flops 33816576 | bytes 8978944 | tf_op jit(solution)/shard_map/bkgj,bjkd->bkgd/dot_general | solution.py:55
  65.7 0.3 fusion.12
  66.1 10.1 %psum.29 = f32[16,2,4]{2,1,0:T(2,128)S(1)} all-reduce(f32[16,2,4]{2,1,0:T(2,128)S(1)} %fusion.12), channel_id=1, replica_groups=mesh['dp'=2,'tp'=4,'sp'=4] {'sp'}, use_global_device_ids=true, to_apply=%region_5.6 | all-reduce | flops 128 | bytes 1024 | tf_op jit(solution)/shard_map/psum | solution.py:54
  76.2 21.4 %all-reduce.4.cloned.1.call-done = f32[16,2,4,128]{3,2,1,0:T(4,128)} async-done(((f32[16,2,4,128]{3,2,1,0:T(4,128)}), f32[16,2,4,128]{3,2,1,0:T(4,128)}) %all-reduce.4.cloned.1.call-update) | async-done | bytes 65552 | tf_op jit(solution)/shard_map/psum | solution.py:55
  97.6 0.9 divide_convert_fusion
  98.6 5.3 %fusion.5 = f32[16,4096]{1,0:T(8,128)} fusion(bf16[16,1024]{1,0:T(8,128)(2,1)S(1)} %reshape.248, bf16[1024,4096]{1,0:T(8,128)(2,1)} %param.15), kind=kOutput, calls=%fused_computation.9 | convolution fusion | flops 134348800 | bytes 8683520 | tf_op jit(solution)/shard_map/dot_general | solution.py:60
  103.9 0.2 all-reduce.8.cloned.1.call-start
  104.1 35.4 %all-reduce.6.cloned.1.call-done = f32[16,4096]{1,0:T(8,128)} async-done(((f32[16,4096]{1,0:T(8,128)}), f32[16,4096]{1,0:T(8,128)}) %all-reduce.6.cloned.1.call-update) | async-done | bytes 262160 | tf_op jit(solution)/shard_map/psum | solution.py:61
  139.5 1.1 multiply_reduce_fusion
  140.6 20.8 %fusion.20 = f32[16,7168]{1,0:T(8,128)S(1)} fusion(bf16[4096,7168]{1,0:T(8,128)(2,1)} %param.16, f32[4096]{0:T(1024)S(1)} %copy-done.3, f32[16]{0:T(128)S(1)} %add_rsqrt_fusion, f32[16,4096]{1,0:T(8,128)} %all-reduce.6.cloned.1.call-done, bf16[16,4096]{1,0:T(8,128)(2,1)S(1)} %copy-done.1), kind=kOutput, calls=%fused_computation.27 | convolution fusion | flops 939851776 | bytes 59588672 | tf_op jit(solution)/shard_map/dot_general | solution.py:63
  161.4 12.1 %fusion.4 = f32[16,4096]{1,0:T(8,128)} fusion(bf16[3584,4096]{1,0:T(8,128)(2,1)} %param.17, f32[16,7168]{1,0:T(8,128)S(1)} %fusion.20), kind=kOutput, calls=%fused_computation.7 | convolution fusion | flops 470237184 | bytes 30081024 | tf_op jit(solution)/shard_map/dot_general | solution.py:66
  173.5 35.4 %all-reduce.8.cloned.1.call-done = f32[16,4096]{1,0:T(8,128)} async-done(((f32[16,4096]{1,0:T(8,128)}), f32[16,4096]{1,0:T(8,128)}) %all-reduce.8.cloned.1.call-update) | async-done | bytes 262160 | tf_op jit(solution)/shard_map/psum | solution.py:67
  208.9 1.6 add_convert_fusion
  (26 shorter events, 0.4 us)
Async XLA Ops:
  7.2 90.4 %all-reduce.4.cloned.1.call-start = ((), (), s32[]{:S(2)}) async-start(), calls=%async_computation | async-start | bytes 131072 | tf_op jit(solution)/shard_map/psum | solution.py:55
  8.3 6.7 %copy-start.4 = (s32[16]{0:T(128)S(1)}, s32[16]{0:T(128)}, u32[]{:S(2)}) copy-start(s32[16]{0:T(128)} %param.11) | copy-start | bytes 196
  41.7 3.4 %copy-start = (bf16[16,1024,2,128]{3,2,1,0:T(2,128)(2,1)}, bf16[16,1024,2,128]{3,2,1,0:T(2,128)(2,1)S(1)}, u32[]{:S(2)}) copy-start(bf16[16,1024,2,128]{3,2,1,0:T(2,128)(2,1)S(1)} %get-tuple-element.5) | copy-start | bytes 25165828
  65.7 73.8 %copy-start.1 = (bf16[16,4096]{1,0:T(8,128)(2,1)S(1)}, bf16[16,4096]{1,0:T(8,128)(2,1)}, u32[]{:S(2)}) copy-start(bf16[16,4096]{1,0:T(8,128)(2,1)} %param.10) | copy-start | bytes 393220
  65.7 74.9 %copy-start.3 = (f32[4096]{0:T(1024)S(1)}, f32[4096]{0:T(1024)}, u32[]{:S(2)}) copy-start(f32[4096]{0:T(1024)} %param.13) | copy-start | bytes 49156
  65.7 73.8 %all-reduce.6.cloned.1.call-start = ((), (), s32[]{:S(2)}) async-start(), calls=%async_computation.1 | async-start | bytes 524288 | tf_op jit(solution)/shard_map/psum | solution.py:61
  103.9 105.0 %all-reduce.8.cloned.1.call-start = ((), (), s32[]{:S(2)}) async-start(), calls=%async_computation.2 | async-start | bytes 524288 | tf_op jit(solution)/shard_map/psum | solution.py:67
  161.4 47.5 %copy-start.2 = (f32[16,4096]{1,0:T(8,128)S(1)}, f32[16,4096]{1,0:T(8,128)}, u32[]{:S(2)}) copy-start(f32[16,4096]{1,0:T(8,128)} %all-reduce.6.cloned.1.call-done) | copy-start | bytes 786436
Sparse Core Ops, SparseCore 0:
  65.8 31.7 all-reduce.3
  104.0 35.4 all-reduce.5
  173.6 35.1 all-reduce.7
where the time goes:
time: 217 us
  waiting for transfers between devices  92.1 us (42%)
  matrix products  52.5 us (24%)
  other arithmetic  31.8 us (15%)
  blocking collectives  22.9 us (11%)
  between operations  13.9 us (6%)
  local copies, waits for them, and re-layouts  3.51 us (2%)
    psum x1, waiting for transfers between devices, layer_tail(): result = mid_resid + lax.psum(down_part, 'tp')  35.4 us
    psum x1, waiting for transfers between devices, layer_tail(): mid_resid = resid_in + lax.psum(out_part, 'tp')  35.4 us
    select_n x1, other arithmetic, write_entry(): return jnp.where(at_slot, entry[:, None], cache)  26.2 us
    psum x1, waiting for transfers between devices, window_attention(): lax.psum(jnp.einsum('bkgj,bjkd->bkgd', weights.astype(jnp.bfloat16), v_bl...  21.4 us
    dot_general x1, matrix products, layer_tail(): gate_up = jnp.dot(normed_mlp, w_gate_up, preferred_element_type=jnp.float32)  20.8 us
    pmax x1, blocking collectives, window_attention(): glob_max = lax.pmax(jnp.max(scores, axis=-1), 'sp')  12.7 us
    dot_general x1, matrix products, layer_tail(): jnp.dot(act_vals, w_down, preferred_element_type=jnp.float32)  12.1 us
    psum x1, blocking collectives, window_attention(): weight_sum = lax.psum(jnp.sum(weights, axis=-1), 'sp')  10.1 us
  transfers between devices with their start and end apart: 3, of which 3 were waited for; matrix products, arithmetic and copies ran while one was open for 0% of the time, Pallas kernels for 0%

commit v1 on v0

v1 whole, which is shorter than its diff:
```python
import functools

import jax
import jax.numpy as jnp
from jax import lax
from jax.experimental import pallas as pl
from jax.experimental.pallas import tpu as pltpu
from jax.sharding import PartitionSpec as P

WINDOW = 2047
ROPE_BASE = 10000.0
NORM_EPS = 1e-5
MESH = pl.DeviceIdType.MESH
F32 = jnp.float32
BF16 = jnp.bfloat16
NEG = float(jnp.finfo(jnp.float32).min)

TP = 4
SP = 4
W_CHUNKS = 8
GROUP = 4
OFFSETS = (
    (0, 1), (0, 2), (0, 3), (1, 0), (1, 1), (2, 0), (2, 1), (1, 2), (1, 3),
    (3, 0), (3, 1), (2, 2), (2, 3), (3, 2), (3, 3),
)


def rope_tables(positions, head_dim):
    inv_freq = ROPE_BASE ** (-jnp.arange(0, head_dim, 2).astype(F32) / head_dim)
    angles = positions.astype(F32)[:, None] * inv_freq[None, :]
    cos, sin = jnp.cos(angles), jnp.sin(angles)
    return jnp.concatenate([cos, cos], axis=-1), jnp.concatenate([-sin, sin], axis=-1)


def attend_kernel(
    ploc_ref, x_ref, gain_ref, cos_ref, sin_ref, wq_ref, k_ref, v_ref,
    k_out, v_out, part_ref,
    k_buf, v_buf, w_buf, r_buf, q_buf, kn_buf, vn_buf, w_sem, k_sem, v_sem, ko_sem, vo_sem,
):
    rows, dim = x_ref.shape
    keys = k_ref.shape[1]
    depth = dim // W_CHUNKS

    def w_copy(c):
        return pltpu.make_async_copy(wq_ref.at[pl.ds(c * depth, depth)], w_buf.at[c], w_sem.at[c])

    def k_copy(b):
        return pltpu.make_async_copy(k_ref.at[b], k_buf.at[b], k_sem.at[b])

    def v_copy(b):
        return pltpu.make_async_copy(v_ref.at[b], v_buf.at[b], v_sem.at[b])

    def k_back(b):
        return pltpu.make_async_copy(k_buf.at[b], k_out.at[b], ko_sem.at[b])

    def v_back(b):
        return pltpu.make_async_copy(v_buf.at[b], v_out.at[b], vo_sem.at[b])

    for c in range(W_CHUNKS):
        w_copy(c).start()
    for b in range(rows):
        k_copy(b).start()
        v_copy(b).start()

    x = x_ref[...].astype(F32)
    scale = lax.rsqrt(jnp.mean(x * x, axis=-1, keepdims=True) + NORM_EPS)
    r_buf[...] = (x * scale * gain_ref[...]).astype(BF16)
    qkv = None
    for c in range(W_CHUNKS):
        w_copy(c).wait()
        term = jnp.dot(r_buf[:, c * depth:(c + 1) * depth], w_buf[c], preferred_element_type=F32)
        qkv = term if qkv is None else qkv + term

    cos, sin = cos_ref[...], sin_ref[...]

    def rotate(vals):
        out = vals * cos + pltpu.roll(vals, 64, 1) * sin
        return out.astype(BF16).astype(F32)

    for kv in range(2):
        base = kv * 768
        for h in range(4):
            q_buf[:, kv * 4 + h, :] = rotate(qkv[:, base + h * 128:base + (h + 1) * 128])
        kn_buf[kv] = rotate(qkv[:, base + 512:base + 640])
        vn_buf[kv] = qkv[:, base + 640:base + 768].astype(BF16).astype(F32)

    lane = lax.broadcasted_iota(jnp.int32, (8, keys), 1)
    head = lax.broadcasted_iota(jnp.int32, (8, keys), 0)
    own = (lane & 1) == (head >> 2)
    slot = lane >> 1
    row16 = lax.broadcasted_iota(jnp.int32, (16, 128), 0)
    stat_col = lax.broadcasted_iota(jnp.int32, (8, 128), 1)
    stat_row = lax.broadcasted_iota(jnp.int32, (8, 128), 0)

    def put(ref, new_buf, b, ploc):
        start = pl.multiple_of((jnp.clip(ploc * 2, 0, keys - 2) // 16) * 16, 16)
        block = ref[b, pl.ds(start, 16), :].astype(F32)
        first = new_buf[0, pl.ds(b, 1), :]
        second = new_buf[1, pl.ds(b, 1), :]
        at = row16 + start
        block = jnp.where(at == ploc * 2, first, block)
        block = jnp.where(at == ploc * 2 + 1, second, block)
        ref[b, pl.ds(start, 16), :] = block.astype(BF16)

    def group(g, carry):
        m_all, l_all = carry
        ids = [g * GROUP + i for i in range(GROUP)]
        plocs = [ploc_ref[b] for b in ids]
        scores, masks = [], []
        for b, ploc in zip(ids, plocs):
            k_copy(b).wait()
            put(k_buf, kn_buf, b, ploc)
            k_back(b).start()
            s = lax.dot_general(
                q_buf[b].astype(BF16), k_buf[b], (((1,), (1,)), ((), ())), preferred_element_type=F32
            )
            scores.append(s)
        probs, sums = [], []
        for b, ploc, s in zip(ids, plocs, scores):
            mask = own & (slot <= ploc) & (slot >= ploc - WINDOW)
            s = jnp.where(mask, s * (128 ** -0.5), NEG)
            m = jnp.max(s, axis=-1, keepdims=True)
            w = jnp.where(mask, jnp.exp(s - m), 0.0)
            l = jnp.sum(w, axis=-1, keepdims=True)
            at = stat_col == b * 8 + stat_row
            m_all = jnp.where(at, m, m_all)
            l_all = jnp.where(at, l, l_all)
            probs.append(w.astype(BF16))
        for b, ploc, w in zip(ids, plocs, probs):
            v_copy(b).wait()
            put(v_buf, vn_buf, b, ploc)
            v_back(b).start()
            part_ref[b] = jnp.dot(w, v_buf[b], preferred_element_type=F32)
        return m_all, l_all

    zero = jnp.zeros((8, 128), F32)
    m_all, l_all = lax.fori_loop(0, rows // GROUP, group, (zero, zero))
    part_ref[rows] = m_all
    part_ref[rows + 1] = l_all
    for b in range(rows):
        k_back(b).wait()
        v_back(b).wait()


def layer_kernel(
    part_ref, x_ref, gain_ref, wo_ref, wg_ref, wd_ref, out_ref,
    wo_buf, wg_buf, wd_buf, part_rx, o_buf, ob_buf, rs_tx, rs_rx, ag_buf, ss_buf,
    act_buf, rs2_tx, rs2_rx, ag2_buf,
    wo_sem, wg_sem, wd_sem, a_sem, b_sem, s_sem, g_sem, c_sem, d_sem, e_sem,
):
    dp, t, s = lax.axis_index("dp"), lax.axis_index("tp"), lax.axis_index("sp")
    rows = x_ref.shape[0]
    units = wg_buf.shape[1] // 2
    ffn = wd_ref.shape[0]
    me = s * TP + t

    def peer(off):
        return (dp, t ^ off[0], s ^ off[1])

    def piece_of(off):
        return (s ^ off[1]) * TP + (t ^ off[0])

    def remote(src, dst, sems, k, off):
        return pltpu.make_async_remote_copy(
            src_ref=src, dst_ref=dst, send_sem=sems.at[0, k], recv_sem=sems.at[1, k],
            device_id=peer(off), device_id_type=MESH,
        )

    loads_o = []
    for d in range(TP):
        col = pl.multiple_of((s * TP + d) * 256, 256)
        loads_o.append(pltpu.make_async_copy(wo_ref.at[:, pl.ds(col, 256)], wo_buf.at[d], wo_sem.at[d]))
    loads_g = []
    for c in range(8):
        for half in range(2):
            col = pl.multiple_of(half * ffn + s * units, 128)
            loads_g.append(pltpu.make_async_copy(
                wg_ref.at[pl.ds(c * 512, 512), pl.ds(col, units)],
                wg_buf.at[pl.ds(c * 512, 512), pl.ds(half * units, units)],
                wg_sem.at[c, half],
            ))
    loads_d = []
    for c in range(SP):
        col = pl.multiple_of(s * 1024, 1024)
        loads_d.append(pltpu.make_async_copy(
            wd_ref.at[pl.ds(c * units, units), pl.ds(col, 1024)], wd_buf.at[c], wd_sem.at[c]
        ))
    for copy in loads_o + loads_g + loads_d:
        copy.start()

    barrier = pltpu.get_barrier_semaphore()
    for off in OFFSETS:
        pl.semaphore_signal(barrier, inc=1, device_id=peer(off), device_id_type=MESH)
    pl.semaphore_wait(barrier, len(OFFSETS))

    sends = []
    for k in (2, 1, 0):
        copy = remote(part_ref, part_rx.at[k], a_sem, k, (0, k + 1))
        copy.start()
        sends.append(copy)
    for copy in sends:
        copy.wait()
    parts = [part_ref, part_rx.at[0], part_rx.at[1], part_rx.at[2]]
    top = None
    for p in parts:
        top = p[rows] if top is None else jnp.maximum(top, p[rows])
    facs = [jnp.exp(p[rows] - top) for p in parts]
    total = sum(p[rows + 1] * f for p, f in zip(parts, facs))
    inv = 1.0 / total
    facs = [f * inv for f in facs]
    lane8 = lax.broadcasted_iota(jnp.int32, (8, 128), 1)
    sub8 = lax.broadcasted_iota(jnp.int32, (8, 128), 0)
    for b in range(rows):
        at = lane8 == sub8 + b * 8
        o = None
        for p, f in zip(parts, facs):
            col = jnp.sum(jnp.where(at, f, 0.0), axis=-1, keepdims=True)
            o = p[b] * col if o is None else o + p[b] * col
        o_buf[b] = o
    for h in range(8):
        ob_buf[:, h * 128:(h + 1) * 128] = o_buf[:, h, :].astype(BF16)

    def reduce_scatter(make_term, tx, rx, sems):
        sends = []
        for dt in (3, 2, 1):
            tx[dt] = make_term(t ^ dt)
            copy = remote(tx.at[dt], rx.at[dt - 1], sems, dt - 1, (dt, 0))
            copy.start()
            sends.append(copy)
        mine = make_term(t)
        for copy in sends:
            copy.wait()
        return mine + rx[0] + rx[1] + rx[2]

    for copy in loads_o:
        copy.wait()
    o_all = ob_buf[...]

    def out_term(d):
        return jnp.dot(o_all, wo_buf[d], preferred_element_type=F32).astype(BF16).astype(F32)

    my_cols = pl.ds(pl.multiple_of(me * 256, 256), 256)
    mid = x_ref[:, my_cols].astype(F32) + reduce_scatter(out_term, rs_tx, rs_rx, b_sem)
    ag_buf[me] = mid
    lane16 = lax.broadcasted_iota(jnp.int32, (rows, 128), 1)
    sub16 = lax.broadcasted_iota(jnp.int32, (rows, 128), 0)
    diag = lane16 == sub16
    sq = jnp.sum(mid * mid, axis=-1, keepdims=True)
    ss_buf[me] = jnp.sum(jnp.where(diag, sq, 0.0), axis=0, keepdims=True)

    order = tuple(reversed(range(len(OFFSETS))))

    def gather_start(buf, sems):
        sends = []
        for k in order:
            copy = remote(buf.at[me], buf.at[me], sems, k, OFFSETS[k])
            copy.start()
            sends.append(copy)
        return sends

    def gather_wait(buf, sems, k):
        slot = piece_of(OFFSETS[k])
        remote(buf.at[slot], buf.at[slot], sems, k, OFFSETS[k]).wait_recv()
        return slot

    ss_sends = gather_start(ss_buf, s_sem)
    ag_sends = gather_start(ag_buf, g_sem)
    for k in range(len(OFFSETS)):
        gather_wait(ss_buf, s_sem, k)
    tot = jnp.sum(ss_buf[...], axis=0)
    mean_sq = jnp.sum(jnp.where(diag, tot, 0.0), axis=-1, keepdims=True) / (16 * 256)
    rstd = lax.rsqrt(mean_sq + NORM_EPS)
    for copy in loads_g:
        copy.wait()
    hid = None
    for k in range(-1, len(OFFSETS)):
        slot = me if k < 0 else gather_wait(ag_buf, g_sem, k)
        at = pl.ds(pl.multiple_of(slot * 256, 256), 256)
        r2 = (ag_buf[slot] * rstd * gain_ref[:, at]).astype(BF16)
        term = jnp.dot(r2, wg_buf[at, :], preferred_element_type=F32)
        hid = term if hid is None else hid + term
    gate, up = hid[:, :units], hid[:, units:]
    act_buf[s] = (gate * jax.nn.sigmoid(gate) * up).astype(BF16).astype(F32)

    act_sends = []
    for k in (2, 1, 0):
        copy = remote(act_buf.at[s], act_buf.at[s], c_sem, k, (0, k + 1))
        copy.start()
        act_sends.append(copy)
    for copy in loads_d:
        copy.wait()
    down = jnp.dot(act_buf[s].astype(BF16), wd_buf[s], preferred_element_type=F32)
    for k in range(3):
        slot = s ^ (k + 1)
        remote(act_buf.at[slot], act_buf.at[slot], c_sem, k, (0, k + 1)).wait_recv()
        down = down + jnp.dot(act_buf[slot].astype(BF16), wd_buf[slot], preferred_element_type=F32)
    down = down.astype(BF16).astype(F32)
    for d in range(TP):
        rs2_tx[d] = down[:, d * 256:(d + 1) * 256]
    sends = []
    for dt in (3, 2, 1):
        copy = remote(rs2_tx.at[t ^ dt], rs2_rx.at[dt - 1], d_sem, dt - 1, (dt, 0))
        copy.start()
        sends.append(copy)
    for copy in sends:
        copy.wait()
    ag2_buf[me] = mid + (rs2_tx[t] + rs2_rx[0] + rs2_rx[1] + rs2_rx[2])
    ag2_sends = gather_start(ag2_buf, e_sem)
    for k in range(len(OFFSETS)):
        gather_wait(ag2_buf, e_sem, k)
    for i in range(16):
        out_ref[:, i * 256:(i + 1) * 256] = ag2_buf[i].astype(BF16)
    for copy in ss_sends + ag_sends + act_sends + ag2_sends:
        copy.wait_send()


def solution(mesh):
    cache_spec = P("dp", "sp", "tp", None)
    vmem = pl.BlockSpec(memory_space=pltpu.VMEM)
    smem = pl.BlockSpec(memory_space=pltpu.SMEM)
    hbm = pl.BlockSpec(memory_space=pltpu.HBM)

    def local_step(hidden, positions, norm_attn, norm_mlp, w_qkv, w_out, w_gate_up, w_down, k_cache, v_cache):
        rows, block_len, kv_local, head_dim = k_cache.shape
        dim = hidden.shape[1]
        keys = block_len * kv_local
        ploc = positions - lax.axis_index("sp") * block_len
        cos, sin = rope_tables(positions, head_dim)
        flat = (rows, keys, head_dim)
        k_upd, v_upd, part = pl.pallas_call(
            attend_kernel,
            out_shape=(
                jax.ShapeDtypeStruct(flat, BF16),
                jax.ShapeDtypeStruct(flat, BF16),
                pltpu.VMEM((rows + 2, 8, 128), F32),
            ),
            in_specs=[smem, vmem, vmem, vmem, vmem, hbm, hbm, hbm],
            out_specs=(hbm, hbm, vmem),
            scratch_shapes=[
                pltpu.VMEM(flat, BF16),
                pltpu.VMEM(flat, BF16),
                pltpu.VMEM((W_CHUNKS, dim // W_CHUNKS, w_qkv.shape[1]), BF16),
                pltpu.VMEM((rows, dim), BF16),
                pltpu.VMEM((rows, 8, 128), F32),
                pltpu.VMEM((2, rows, 128), F32),
                pltpu.VMEM((2, rows, 128), F32),
                pltpu.SemaphoreType.DMA((W_CHUNKS,)),
                pltpu.SemaphoreType.DMA((rows,)),
                pltpu.SemaphoreType.DMA((rows,)),
                pltpu.SemaphoreType.DMA((rows,)),
                pltpu.SemaphoreType.DMA((rows,)),
            ],
            compiler_params=pltpu.CompilerParams(vmem_limit_bytes=62 * 2 ** 20),
            cost_estimate=pl.CostEstimate(flops=10 ** 9, bytes_accessed=3 * 10 ** 7, transcendentals=10 ** 6),
        )(ploc, hidden, norm_attn.reshape(1, dim), cos, sin, w_qkv, k_cache.reshape(flat), v_cache.reshape(flat))
        units = w_down.shape[0] // SP
        result = pl.pallas_call(
            layer_kernel,
            out_shape=jax.ShapeDtypeStruct((rows, dim), BF16),
            in_specs=[vmem, vmem, vmem, hbm, hbm, hbm],
            out_specs=vmem,
            scratch_shapes=[
                pltpu.VMEM((TP, 1024, 256), BF16),
                pltpu.VMEM((dim, 2 * units), BF16),
                pltpu.VMEM((SP, units, 1024), BF16),
                pltpu.VMEM((3, rows + 2, 8, 128), F32),
                pltpu.VMEM((rows, 8, 128), F32),
                pltpu.VMEM((rows, 1024), BF16),
                pltpu.VMEM((TP, rows, 256), F32),
                pltpu.VMEM((3, rows, 256), F32),
                pltpu.VMEM((16, rows, 256), F32),
                pltpu.VMEM((16, 1, 128), F32),
                pltpu.VMEM((SP, rows, units), F32),
                pltpu.VMEM((TP, rows, 256), F32),
                pltpu.VMEM((3, rows, 256), F32),
                pltpu.VMEM((16, rows, 256), F32),
                pltpu.SemaphoreType.DMA((TP,)),
                pltpu.SemaphoreType.DMA((8, 2)),
                pltpu.SemaphoreType.DMA((SP,)),
                pltpu.SemaphoreType.DMA((2, 3)),
                pltpu.SemaphoreType.DMA((2, 3)),
                pltpu.SemaphoreType.DMA((2, 15)),
                pltpu.SemaphoreType.DMA((2, 15)),
                pltpu.SemaphoreType.DMA((2, 3)),
                pltpu.SemaphoreType.DMA((2, 3)),
                pltpu.SemaphoreType.DMA((2, 15)),
            ],
            compiler_params=pltpu.CompilerParams(
                collective_id=0, has_side_effects=True, vmem_limit_bytes=62 * 2 ** 20
            ),
            cost_estimate=pl.CostEstimate(flops=4 * 10 ** 9, bytes_accessed=3 * 10 ** 7, transcendentals=10 ** 6),
        )(part, hidden, norm_mlp.reshape(1, dim), w_out, w_gate_up, w_down)
        return result, k_upd.reshape(k_cache.shape), v_upd.reshape(v_cache.shape)

    return jax.shard_map(
        local_step, mesh=mesh,
        in_specs=(P("dp", None), P("dp"), P(None), P(None), P(None, "tp"), P("tp", None), P(None, "tp"), P("tp", None), cache_spec, cache_spec),
        out_specs=(P("dp", None), cache_spec, cache_spec), check_vma=False,
    )
```

time: 217 us -> 66.9 us (0.31)
  waiting for transfers between devices: 92.1 us -> 0 us
  Pallas kernels: 0 us -> 61.8 us
  matrix products: 52.5 us -> 0 us
  other arithmetic: 31.8 us -> 2.04 us
  blocking collectives: 22.9 us -> 0 us
  between operations: 13.9 us -> 0.67 us
    psum x3 -> x0, waiting for transfers between devices: 92.1 us -> none  [the longest x1 35.4 us: layer_tail(): result = mid_resid + lax.psum(down_part, 'tp')]
    pallas_call x0 -> x2, Pallas kernels: none -> 61.8 us  [the longest x1 42.1 us: local_step(): pl.pallas_call(layer_kernel, out_shape=jax.ShapeDtypeStruct((rows, dim),...]
    dot_general x6 -> x0, matrix products: 52.5 us -> none  [the longest x1 20.8 us: layer_tail(): gate_up = jnp.dot(normed_mlp, w_gate_up, preferred_element_type=jnp.float32)]
    select_n x1 -> x0, other arithmetic: 26.2 us -> none  [write_entry(): return jnp.where(at_slot, entry[:, None], cache)]
    pmax x1 -> x0, blocking collectives: 12.7 us -> none  [window_attention(): glob_max = lax.pmax(jnp.max(scores, axis=-1), 'sp')]
    psum x1 -> x0, blocking collectives: 10.1 us -> none  [window_attention(): weight_sum = lax.psum(jnp.sum(weights, axis=-1), 'sp')]
    reduce_sum x3 -> x0, other arithmetic: 2.49 us -> none  [the longest x2 2.15 us: rms_norm(): mean_sq = jnp.mean(values * values, axis=-1, keepdims=True)]
  transfers between devices with their start and end apart: 3 -> 0, of which waited for: 3 -> 0; matrix products, arithmetic and copies ran while one was open for 0% -> 0% of each run, Pallas kernels for 0% -> 0%
where the time goes in v1:
time: 66.9 us; the launch traced here: 66.8 us
  Pallas kernels  61.8 us (92%)
  local copies, waits for them, and re-layouts  2.2 us (3%)
  other arithmetic  2.04 us (3%)
  between operations  0.67 us (1%)
    pallas_call x1, Pallas kernels, local_step(): pl.pallas_call(layer_kernel, out_shape=jax.ShapeDtypeStruct((rows, dim),...  42.1 us
    pallas_call x1, Pallas kernels, local_step(): pl.pallas_call(attend_kernel, out_shape=(jax.ShapeDtypeStruct(flat, BF16)...  19.7 us
    unnamed x3, local copies, waits for them, and re-layouts  2.2 us

profile of v1, /device:TPU:0, one launch (start us, length us, event | category | flops | bytes accessed | tf_op | source)
XLA Modules:
  0.0 66.8 jit_solution(17821668239781373962)
XLA Ops:
  0.6 1.2 %fusion.1 = (f32[16]{0:T(128)S(1)}, s32[16]{0:T(128)}) fusion(s32[16]{0:T(128)} %param.11, s32[]{:T(128)S(6)} %mul.26), kind=kLoop, calls=%fused_computation.7 | loop fusion | flops 32 | bytes 196 | tf_op jit(solution)/shard_map/convert_element_type | solution.py:30
  1.9 0.1 fusion
  2.0 0.7 %pad_maximum_fusion = (f32[16,128]{1,0:T(8,128)}, f32[16,128]{1,0:T(8,128)}) fusion(f32[16,64]{1,0:T(8,128)S(1)} %get-tuple-element.11, f32[16,64]{1,0:T(8,128)S(1)} %get-tuple-element.10, f32[16,64]{1,0:T(8,128)S(1)} %get-tuple-element.9), kind=kLoop, calls=%fused_computation.2 | loop fusion | flops 4096 | bytes 28672 | tf_op jit(solution)/shard_map/concatenate | solution.py:32
  2.7 19.7 %shard_map.121 = (bf16[16,2048,128]{2,1,0:T(8,128)(2,1)}, bf16[16,2048,128]{2,1,0:T(8,128)(2,1)}, f32[18,8,128]{2,1,0:T(8,128)S(1)}) custom-call(s32[16]{0:T(128)} %get-tuple-element.13.ploc_ref, bf16[16,4096]{1,0:T(8,128)(2,1)} %x_ref.3, f32[1,4096]{1,0:T(1,128)} %bitcast.8, f32[16,128]{1,0:T(8,128)} %get-tuple-element.14.cos_ref, ...), custom_call_target="tpu_custom_call" | custom-call | flops 1000000000 | bytes 30000000 | tf_op jit(solution)/shard_map/pallas_call | solution.py:330
  22.4 0.0 copy-start
  22.4 0.6 copy-done
  23.1 42.1 %shard_map.122 = bf16[16,4096]{1,0:T(8,128)(2,1)} custom-call(f32[18,8,128]{2,1,0:T(8,128)} %copy-done, bf16[16,4096]{1,0:T(8,128)(2,1)} %x_ref.3, f32[1,4096]{1,0:T(1,128)} %bitcast.9, bf16[1024,4096]{1,0:T(8,128)(2,1)} %wo_ref.1, bf16[4096,7168]{1,0:T(8,128)(2,1)} %wg_ref.1, bf16[3584,4096]{1,0:T(8,128)(2,1)} %wd_ref.1), custom_call_target="tpu_custom_call" | custom-call | flops 4000000000 | bytes 30000000 | tf_op jit(solution)/shard_map/pallas_call | solution.py:357
  65.2 1.6 %copy.14 = bf16[16,4096]{1,0:T(8,128)(2,1)} copy(bf16[16,4096]{1,0:T(8,128)(2,1)} %shard_map.122) | data formatting | bytes 262144
  (1 shorter events, 0.0 us)
Async XLA Ops:
  22.4 0.6 copy-start

commit v2 on v1

v2 whole, which is shorter than its diff:
```python
import jax
import jax.numpy as jnp
import numpy as np
from jax import lax
from jax.experimental import pallas as pl
from jax.experimental.pallas import tpu as pltpu
from jax.sharding import PartitionSpec as P

WINDOW = 2047
ROPE_BASE = 10000.0
NORM_EPS = 1e-5
MESH = pl.DeviceIdType.MESH
F32 = jnp.float32
BF16 = jnp.bfloat16
NEG = float(jnp.finfo(jnp.float32).min)

TP = 4
SP = 4
W_CHUNKS = 8
GROUP = 4
OFFSETS = (
    (0, 1), (0, 3), (0, 2), (1, 1), (1, 0), (1, 3), (1, 2), (2, 1), (2, 0),
    (2, 3), (2, 2), (3, 1), (3, 0), (3, 3), (3, 2),
)
VIA = {off: off if off[1] & 1 else (0, 1) for off in OFFSETS}


def add_offsets(a, b):
    return (a[0] ^ b[0], a[1] ^ b[1])


def attend_kernel(
    pos_ref, freq_ref, x_ref, gain_ref, wq_ref, k_ref, v_ref,
    k_out, v_out, part_ref,
    pos, freq, x_buf, gain, k_buf, v_buf, w_buf, r_buf, q_buf, kn_buf, vn_buf,
    in_sem, w_sem, k_sem, v_sem, ko_sem, vo_sem,
):
    rows, dim = x_ref.shape
    keys = k_ref.shape[1]
    depth = dim // W_CHUNKS

    def w_copy(c):
        return pltpu.make_async_copy(wq_ref.at[pl.ds(c * depth, depth)], w_buf.at[c], w_sem.at[c])

    def k_copy(b):
        return pltpu.make_async_copy(k_ref.at[b], k_buf.at[b], k_sem.at[b])

    def v_copy(b):
        return pltpu.make_async_copy(v_ref.at[b], v_buf.at[b], v_sem.at[b])

    def k_back(b):
        return pltpu.make_async_copy(k_buf.at[b], k_out.at[b], ko_sem.at[b])

    def v_back(b):
        return pltpu.make_async_copy(v_buf.at[b], v_out.at[b], vo_sem.at[b])

    small = [
        pltpu.make_async_copy(src, dst, in_sem.at[i])
        for i, (src, dst) in enumerate(((x_ref, x_buf), (gain_ref, gain), (freq_ref, freq), (pos_ref, pos)))
    ]
    for copy in small:
        copy.start()
    for c in range(W_CHUNKS):
        w_copy(c).start()
    small[0].wait()
    small[1].wait()
    x = x_buf[...].astype(F32)
    scale = lax.rsqrt(jnp.mean(x * x, axis=-1, keepdims=True) + NORM_EPS)
    r_buf[...] = (x * scale * gain[...]).astype(BF16)
    small[2].wait()
    small[3].wait()
    row_id = lax.broadcasted_iota(jnp.int32, (rows, 128), 0)
    lane_id = lax.broadcasted_iota(jnp.int32, (rows, 128), 1)
    pos_col = jnp.zeros((rows, 128), jnp.int32)
    for b in range(rows):
        pos_col = jnp.where(row_id == b, pos[b], pos_col)
    angle = pos_col.astype(F32) * freq[...]
    cos = jnp.cos(angle)
    sin = jnp.where(lane_id < 64, -jnp.sin(angle), jnp.sin(angle))

    per = rows // W_CHUNKS
    qkv = None
    for c in range(W_CHUNKS):
        w_copy(c).wait()
        for b in range(c * per, (c + 1) * per):
            k_copy(b).start()
            v_copy(b).start()
        term = jnp.dot(r_buf[:, c * depth:(c + 1) * depth], w_buf[c], preferred_element_type=F32)
        qkv = term if qkv is None else qkv + term

    def rotate(vals):
        out = vals * cos + pltpu.roll(vals, 64, 1) * sin
        return out.astype(BF16).astype(F32)

    for kv in range(2):
        base = kv * 768
        for h in range(4):
            q_buf[:, kv * 4 + h, :] = rotate(qkv[:, base + h * 128:base + (h + 1) * 128])
        kn_buf[kv] = rotate(qkv[:, base + 512:base + 640])
        vn_buf[kv] = qkv[:, base + 640:base + 768].astype(BF16).astype(F32)

    first_slot = lax.axis_index("sp") * (keys // 2)
    lane = lax.broadcasted_iota(jnp.int32, (8, keys), 1)
    head = lax.broadcasted_iota(jnp.int32, (8, keys), 0)
    own = (lane & 1) == (head >> 2)
    slot = lane >> 1
    row16 = lax.broadcasted_iota(jnp.int32, (16, 128), 0)
    stat_col = lax.broadcasted_iota(jnp.int32, (8, 128), 1)
    stat_row = lax.broadcasted_iota(jnp.int32, (8, 128), 0)

    def put(ref, new_buf, b, ploc):
        start = pl.multiple_of((jnp.clip(ploc * 2, 0, keys - 2) // 16) * 16, 16)
        block = ref[b, pl.ds(start, 16), :].astype(F32)
        first = new_buf[0, pl.ds(b, 1), :]
        second = new_buf[1, pl.ds(b, 1), :]
        at = row16 + start
        block = jnp.where(at == ploc * 2, first, block)
        block = jnp.where(at == ploc * 2 + 1, second, block)
        ref[b, pl.ds(start, 16), :] = block.astype(BF16)

    def stage(b):
        ploc = pos[b] - first_slot
        k_copy(b).wait()
        put(k_buf, kn_buf, b, ploc)
        k_back(b).start()
        v_copy(b).wait()
        put(v_buf, vn_buf, b, ploc)
        v_back(b).start()

    def compute(g, carry):
        m_all, l_all = carry
        ids = [g * GROUP + i for i in range(GROUP)]
        plocs = [pos[b] - first_slot for b in ids]
        scores = [
            lax.dot_general(
                q_buf[b].astype(BF16), k_buf[b], (((1,), (1,)), ((), ())), preferred_element_type=F32
            )
            for b in ids
        ]
        probs = []
        for b, ploc, s in zip(ids, plocs, scores):
            mask = own & (slot <= ploc) & (slot >= ploc - WINDOW)
            s = jnp.where(mask, s * (128 ** -0.5), NEG)
            m = jnp.max(s, axis=-1, keepdims=True)
            w = jnp.where(mask, jnp.exp(s - m), 0.0)
            l = jnp.sum(w, axis=-1, keepdims=True)
            at = stat_col == b * 8 + stat_row
            m_all = jnp.where(at, m, m_all)
            l_all = jnp.where(at, l, l_all)
            probs.append(w.astype(BF16))
        for b, w in zip(ids, probs):
            part_ref[b] = jnp.dot(w, v_buf[b], preferred_element_type=F32)
        return m_all, l_all

    def group(g, carry):
        for i in range(GROUP):
            stage((g + 1) * GROUP + i)
        return compute(g, carry)

    for b in range(GROUP):
        stage(b)
    zero = jnp.zeros((8, 128), F32)
    last = rows // GROUP - 1
    carry = lax.fori_loop(0, last, group, (zero, zero))
    m_all, l_all = compute(last, carry)
    part_ref[rows] = m_all
    part_ref[rows + 1] = l_all
    for b in range(rows):
        k_back(b).wait()
        v_back(b).wait()


def layer_kernel(
    part_ref, x_ref, gain_ref, wo_ref, wg_ref, wd_ref, out_ref,
    x_buf, gain, wo_buf, wg_buf, wd_buf, part_rx, o_buf, ob_buf, rs_tx, rs_rx, ag_buf, ss_buf,
    act_buf, dn_buf, rs2_tx, rs2_rx, ag2_buf,
    in_sem, wo_sem, wg_sem, wd_sem, a_sem, b_sem, s_sem, g_sem, c_sem, d_sem, e_sem,
):
    dp, t, s = lax.axis_index("dp"), lax.axis_index("tp"), lax.axis_index("sp")
    rows = x_ref.shape[0]
    units = wg_buf.shape[1] // 2
    ffn = wd_ref.shape[0]

    def peer(off):
        return (dp, t ^ off[0], s ^ off[1])

    def piece_of(off):
        return (s ^ off[1] ^ 1) * TP + (t ^ off[0])

    me = piece_of((0, 0))

    def remote(src, dst, sems, k, off):
        return pltpu.make_async_remote_copy(
            src_ref=src, dst_ref=dst, send_sem=sems.at[0, k], recv_sem=sems.at[1, k],
            device_id=peer(off), device_id_type=MESH,
        )

    loads_in = [
        pltpu.make_async_copy(x_ref, x_buf, in_sem.at[0]),
        pltpu.make_async_copy(gain_ref, gain, in_sem.at[1]),
    ]
    loads_o = []
    for d in range(TP):
        col = pl.multiple_of((s * TP + d) * 256, 256)
        loads_o.append(pltpu.make_async_copy(wo_ref.at[:, pl.ds(col, 256)], wo_buf.at[d], wo_sem.at[d]))
    loads_g = []
    for c in range(8):
        for half in range(2):
            col = pl.multiple_of(half * ffn + s * units, 128)
            loads_g.append(pltpu.make_async_copy(
                wg_ref.at[pl.ds(c * 512, 512), pl.ds(col, units)],
                wg_buf.at[pl.ds(c * 512, 512), pl.ds(half * units, units)],
                wg_sem.at[c, half],
            ))
    loads_d = []
    for c in range(SP):
        col = pl.multiple_of(s * 1024, 1024)
        loads_d.append(pltpu.make_async_copy(
            wd_ref.at[pl.ds(c * units, units), pl.ds(col, 1024)], wd_buf.at[c], wd_sem.at[c]
        ))
    barrier = pltpu.get_barrier_semaphore()
    for off in OFFSETS:
        pl.semaphore_signal(barrier, inc=1, device_id=peer(off), device_id_type=MESH)
    for copy in loads_in + loads_o + loads_g + loads_d:
        copy.start()
    pl.semaphore_wait(barrier, len(OFFSETS))

    a_sends = []
    for k, off in ((2, (0, 3)), (0, (0, 1))):
        copy = remote(part_ref, part_rx.at[k], a_sem, k, off)
        copy.start()
        a_sends.append(copy)
    remote(part_ref, part_rx.at[2], a_sem, 2, (0, 3)).wait_recv()
    copy = remote(part_rx.at[2], part_rx.at[1], a_sem, 1, (0, 1))
    copy.start()
    a_sends.append(copy)
    for k in range(2):
        remote(part_ref, part_rx.at[k], a_sem, k, (0, 1)).wait_recv()
    parts = [part_ref, part_rx.at[0], part_rx.at[1], part_rx.at[2]]
    top = None
    for p in parts:
        top = p[rows] if top is None else jnp.maximum(top, p[rows])
    facs = [jnp.exp(p[rows] - top) for p in parts]
    total = sum(p[rows + 1] * f for p, f in zip(parts, facs))
    inv = 1.0 / total
    facs = [f * inv for f in facs]
    lane8 = lax.broadcasted_iota(jnp.int32, (8, 128), 1)
    sub8 = lax.broadcasted_iota(jnp.int32, (8, 128), 0)
    for b in range(rows):
        at = lane8 == sub8 + b * 8
        o = None
        for p, f in zip(parts, facs):
            col = jnp.sum(jnp.where(at, f, 0.0), axis=-1, keepdims=True)
            o = p[b] * col if o is None else o + p[b] * col
        o_buf[b] = o
    for h in range(8):
        ob_buf[:, h * 128:(h + 1) * 128] = o_buf[:, h, :].astype(BF16)

    def reduce_scatter(make_term, tx, rx, sems):
        sends = []
        for dt in (3, 2, 1, 0):
            tx[dt] = make_term(t ^ dt)
            copy = remote(tx.at[dt], rx.at[dt], sems, dt, (dt, 1))
            copy.start()
            sends.append(copy)
        for copy in sends:
            copy.wait()
        return rx[0] + rx[1] + rx[2] + rx[3]

    for copy in loads_in + loads_o:
        copy.wait()
    o_all = ob_buf[...]

    def out_term(d):
        return jnp.dot(o_all, wo_buf[d], preferred_element_type=F32).astype(BF16).astype(F32)

    my_cols = pl.ds(pl.multiple_of(me * 256, 256), 256)
    mid = x_buf[:, my_cols].astype(F32) + reduce_scatter(out_term, rs_tx, rs_rx, b_sem)
    ag_buf[me] = mid
    lane16 = lax.broadcasted_iota(jnp.int32, (rows, 128), 1)
    sub16 = lax.broadcasted_iota(jnp.int32, (rows, 128), 0)
    diag = lane16 == sub16
    sq = jnp.sum(mid * mid, axis=-1, keepdims=True)
    ss_buf[me] = jnp.sum(jnp.where(diag, sq, 0.0), axis=0, keepdims=True)

    def broadcast(buf, sems):
        sends = []
        for k in reversed(range(len(OFFSETS))):
            copy = remote(buf.at[me], buf.at[me], sems, k, OFFSETS[k])
            copy.start()
            sends.append(copy)
        return sends

    class Gather:
        def __init__(self, buf, sems):
            self.buf, self.sems, self.sends = buf, sems, []

        def send(self, have):
            for k in reversed(range(len(OFFSETS))):
                off = OFFSETS[k]
                if add_offsets(off, VIA[off]) == have:
                    slot = piece_of(have)
                    copy = remote(self.buf.at[slot], self.buf.at[slot], self.sems, k, VIA[off])
                    copy.start()
                    self.sends.append(copy)

        def wait(self, k, forward=True):
            off = OFFSETS[k]
            slot = piece_of(off)
            remote(self.buf.at[slot], self.buf.at[slot], self.sems, k, VIA[off]).wait_recv()
            if forward:
                self.send(off)
            return slot

    ss_sends = broadcast(ss_buf, s_sem)
    gather = Gather(ag_buf, g_sem)
    gather.send((0, 0))
    for k in range(len(OFFSETS)):
        slot = piece_of(OFFSETS[k])
        remote(ss_buf.at[slot], ss_buf.at[slot], s_sem, k, OFFSETS[k]).wait_recv()
    tot = jnp.sum(ss_buf[...], axis=0)
    mean_sq = jnp.sum(jnp.where(diag, tot, 0.0), axis=-1, keepdims=True) / (16 * 256)
    rstd = lax.rsqrt(mean_sq + NORM_EPS)
    for copy in loads_g:
        copy.wait()
    hid = None
    for k in range(-1, len(OFFSETS)):
        slot = me if k < 0 else gather.wait(k)
        at = pl.ds(pl.multiple_of(slot * 256, 256), 256)
        r2 = (ag_buf[slot] * rstd * gain[:, at]).astype(BF16)
        term = jnp.dot(r2, wg_buf[at, :], preferred_element_type=F32)
        hid = term if hid is None else hid + term
    gate, up = hid[:, :units], hid[:, units:]
    act_buf[s] = (gate * jax.nn.sigmoid(gate) * up).astype(BF16).astype(F32)

    act_sends = []

    def act_send(slot, k, off):
        copy = remote(act_buf.at[slot], act_buf.at[slot], c_sem, k, off)
        copy.start()
        act_sends.append(copy)

    act_send(s, 2, (0, 3))
    act_send(s, 0, (0, 1))
    for copy in loads_d:
        copy.wait()
    down = jnp.dot(act_buf[s].astype(BF16), wd_buf[s], preferred_element_type=F32)
    for k in (0, 2, 1):
        slot = s ^ (k + 1)
        remote(act_buf.at[slot], act_buf.at[slot], c_sem, k, (0, 1)).wait_recv()
        if k == 2:
            act_send(slot, 1, (0, 1))
        down = down + jnp.dot(act_buf[slot].astype(BF16), wd_buf[slot], preferred_element_type=F32)
    rs2_buf = down.astype(BF16).astype(F32)
    for d in range(TP):
        dn_buf[d] = rs2_buf[:, d * 256:(d + 1) * 256]

    def down_term(d):
        return dn_buf[d]

    final = mid + reduce_scatter(down_term, rs2_tx, rs2_rx, d_sem)
    gather2 = Gather(ag2_buf, e_sem)
    gather2.buf[me] = final
    gather2.send((0, 0))
    for k in range(len(OFFSETS)):
        gather2.wait(k)
    for i in range(16):
        out_ref[:, i * 256:(i + 1) * 256] = gather2.buf[i]
    for copy in a_sends + ss_sends + gather.sends + act_sends + gather2.sends:
        copy.wait_send()


def solution(mesh):
    cache_spec = P("dp", "sp", "tp", None)
    vmem = pl.BlockSpec(memory_space=pltpu.VMEM)
    hbm = pl.BlockSpec(memory_space=pltpu.HBM)

    def in_hbm(*arrays):
        return tuple(pltpu.with_memory_space_constraint(a, pltpu.HBM) for a in arrays)

    def local_step(hidden, positions, norm_attn, norm_mlp, w_qkv, w_out, w_gate_up, w_down, k_cache, v_cache):
        rows, block_len, kv_local, head_dim = k_cache.shape
        dim = hidden.shape[1]
        flat = (rows, block_len * kv_local, head_dim)
        freq = ROPE_BASE ** (-np.arange(0, head_dim, 2, dtype=np.float64) / head_dim)
        freq = jnp.asarray(np.concatenate([freq, freq])[None].astype(np.float32))
        k_upd, v_upd, part = pl.pallas_call(
            attend_kernel,
            out_shape=(
                jax.ShapeDtypeStruct(flat, BF16),
                jax.ShapeDtypeStruct(flat, BF16),
                pltpu.VMEM((rows + 2, 8, 128), F32),
            ),
            in_specs=[hbm] * 7,
            out_specs=(hbm, hbm, vmem),
            scratch_shapes=[
                pltpu.SMEM((rows,), jnp.int32),
                pltpu.VMEM((1, head_dim), F32),
                pltpu.VMEM((rows, dim), BF16),
                pltpu.VMEM((1, dim), F32),
                pltpu.VMEM(flat, BF16),
                pltpu.VMEM(flat, BF16),
                pltpu.VMEM((W_CHUNKS, dim // W_CHUNKS, w_qkv.shape[1]), BF16),
                pltpu.VMEM((rows, dim), BF16),
                pltpu.VMEM((rows, 8, 128), F32),
                pltpu.VMEM((2, rows, 128), F32),
                pltpu.VMEM((2, rows, 128), F32),
                pltpu.SemaphoreType.DMA((4,)),
                pltpu.SemaphoreType.DMA((W_CHUNKS,)),
                pltpu.SemaphoreType.DMA((rows,)),
                pltpu.SemaphoreType.DMA((rows,)),
                pltpu.SemaphoreType.DMA((rows,)),
                pltpu.SemaphoreType.DMA((rows,)),
            ],
            compiler_params=pltpu.CompilerParams(vmem_limit_bytes=36 * 2 ** 20),
            cost_estimate=pl.CostEstimate(flops=10 ** 9, bytes_accessed=3 * 10 ** 7, transcendentals=10 ** 6),
        )(*in_hbm(
            positions, freq, hidden, norm_attn.reshape(1, dim), w_qkv, k_cache.reshape(flat), v_cache.reshape(flat)
        ))
        units = w_down.shape[0] // SP
        result = pl.pallas_call(
            layer_kernel,
            out_shape=pltpu.VMEM((rows, dim), F32),
            in_specs=[vmem] + [hbm] * 5,
            out_specs=vmem,
            scratch_shapes=[
                pltpu.VMEM((rows, dim), BF16),
                pltpu.VMEM((1, dim), F32),
                pltpu.VMEM((TP, 1024, 256), BF16),
                pltpu.VMEM((dim, 2 * units), BF16),
                pltpu.VMEM((SP, units, 1024), BF16),
                pltpu.VMEM((3, rows + 2, 8, 128), F32),
                pltpu.VMEM((rows, 8, 128), F32),
                pltpu.VMEM((rows, 1024), BF16),
                pltpu.VMEM((TP, rows, 256), F32),
                pltpu.VMEM((TP, rows, 256), F32),
                pltpu.VMEM((16, rows, 256), F32),
                pltpu.VMEM((16, 1, 128), F32),
                pltpu.VMEM((SP, rows, units), F32),
                pltpu.VMEM((TP, rows, 256), F32),
                pltpu.VMEM((TP, rows, 256), F32),
                pltpu.VMEM((TP, rows, 256), F32),
                pltpu.VMEM((16, rows, 256), F32),
                pltpu.SemaphoreType.DMA((2,)),
                pltpu.SemaphoreType.DMA((TP,)),
                pltpu.SemaphoreType.DMA((8, 2)),
                pltpu.SemaphoreType.DMA((SP,)),
                pltpu.SemaphoreType.DMA((2, 3)),
                pltpu.SemaphoreType.DMA((2, 4)),
                pltpu.SemaphoreType.DMA((2, 15)),
                pltpu.SemaphoreType.DMA((2, 15)),
                pltpu.SemaphoreType.DMA((2, 3)),
                pltpu.SemaphoreType.DMA((2, 4)),
                pltpu.SemaphoreType.DMA((2, 15)),
            ],
            compiler_params=pltpu.CompilerParams(
                collective_id=0, has_side_effects=True, vmem_limit_bytes=32 * 2 ** 20
            ),
            cost_estimate=pl.CostEstimate(flops=4 * 10 ** 9, bytes_accessed=3 * 10 ** 7, transcendentals=10 ** 6),
        )(part, *in_hbm(hidden, norm_mlp.reshape(1, dim), w_out, w_gate_up, w_down))
        return result.astype(BF16), k_upd.reshape(k_cache.shape), v_upd.reshape(v_cache.shape)

    return jax.shard_map(
        local_step, mesh=mesh,
        in_specs=(P("dp", None), P("dp"), P(None), P(None), P(None, "tp"), P("tp", None), P(None, "tp"), P("tp", None), cache_spec, cache_spec),
        out_specs=(P("dp", None), cache_spec, cache_spec), check_vma=False,
    )
```

time: 66.9 us -> 63.1 us (0.943)
  local copies, waits for them, and re-layouts: 2.2 us -> 0 us
  other arithmetic: 2.04 us -> 0.67 us
    pallas_call x1, Pallas kernels: 19.7 us -> 16.4 us  [local_step(): pl.pallas_call(attend_kernel, out_shape=(jax.ShapeDtypeStruct(flat, BF16)...]
    pallas_call x1, Pallas kernels: 42.1 us -> 45.3 us  [local_step(): pl.pallas_call(layer_kernel, out_shape=pltpu.VMEM((rows, dim), F32), in_s...]
    unnamed x3 -> x0, local copies, waits for them, and re-layouts: 2.2 us -> none
    concatenate x1 -> x0, other arithmetic: 0.68 us -> none  [rope_tables(): jnp.concatenate([cos, cos], axis=-1)]
where the time goes in v2:
time: 63.1 us; the launch traced here: 63 us
  Pallas kernels  61.7 us (98%)
  other arithmetic  0.67 us (1%)
  between operations  0.65 us (1%)
    pallas_call x1, Pallas kernels, local_step(): pl.pallas_call(layer_kernel, out_shape=pltpu.VMEM((rows, dim), F32), in_s...  45.3 us
    pallas_call x1, Pallas kernels, local_step(): pl.pallas_call(attend_kernel, out_shape=(jax.ShapeDtypeStruct(flat, BF16)...  16.4 us

profile of v2, /device:TPU:0, one launch (start us, length us, event | category | flops | bytes accessed | tf_op | source)
XLA Modules:
  0.0 63.0 jit_solution(146658135971744593)
XLA Ops:
  0.6 16.4 %shard_map.130 = (bf16[16,2048,128]{2,1,0:T(8,128)(2,1)}, bf16[16,2048,128]{2,1,0:T(8,128)(2,1)}, f32[18,8,128]{2,1,0:T(8,128)S(1)}) custom-call(s32[16]{0:T(128)} %pos_ref.1, f32[1,128]{1,0:T(1,128)} %constant.2.clone.freq_ref, bf16[16,4096]{1,0:T(8,128)(2,1)} %x_ref.3, f32[1,4096]{1,0:T(1,128)} %bitcast.8, bf16[4096,1536]{1,0:T(8,128)(2,1)} %wq_ref.1, ...), custom_call_target="tpu_custom_call" | custom-call | flops 1000000000 | bytes 30000000 | tf_op jit(solution)/shard_map/pallas_call | solution.py:387
  17.0 45.3 %shard_map.131 = f32[16,4096]{1,0:T(8,128)S(1)} custom-call(f32[18,8,128]{2,1,0:T(8,128)S(1)} %get-tuple-element.6.part_ref, bf16[16,4096]{1,0:T(8,128)(2,1)} %x_ref.3, f32[1,4096]{1,0:T(1,128)} %bitcast.9, bf16[1024,4096]{1,0:T(8,128)(2,1)} %wo_ref.1, bf16[4096,7168]{1,0:T(8,128)(2,1)} %wg_ref.1, bf16[3584,4096]{1,0:T(8,128)(2,1)} %wd_ref.1), custom_call_target="tpu_custom_call" | custom-call | flops 4000000000 | bytes 30000000 | tf_op jit(solution)/shard_map/pallas_call | solution.py:421
  62.3 0.7 %convert_element_type.3 = bf16[16,4096]{1,0:T(8,128)(2,1)} convert(f32[16,4096]{1,0:T(8,128)S(1)} %shard_map.131) | non-fusion elementwise | flops 65536 | bytes 393216 | tf_op jit(solution)/shard_map/convert_element_type | solution.py:461

commit v3 on v0

v3 whole, which is shorter than its diff:
```python
import jax
import jax.numpy as jnp
import numpy as np
from jax import lax
from jax.experimental import pallas as pl
from jax.experimental.pallas import tpu as pltpu
from jax.sharding import PartitionSpec as P

WINDOW = 2047
ROPE_BASE = 10000.0
NORM_EPS = 1e-5
MESH = pl.DeviceIdType.MESH
F32 = jnp.float32
BF16 = jnp.bfloat16
NEG = float(jnp.finfo(jnp.float32).min)

TP = 4
SP = 4
W_CHUNKS = 8
GROUP = 4
AHEAD = 4
OFFSETS = (
    (0, 1), (0, 3), (1, 1), (2, 1), (1, 3), (3, 1), (2, 3), (3, 3),
    (0, 2), (1, 0), (2, 0), (1, 2), (3, 0), (2, 2), (3, 2),
)
VIA = {off: off if off[1] & 1 else (0, 1) for off in OFFSETS}


def add_offsets(a, b):
    return (a[0] ^ b[0], a[1] ^ b[1])


def layer_kernel(
    pos_ref, freq_ref, x_ref, gain_ref, gain2_ref, wq_ref, k_ref, v_ref, wo_ref, wg_ref, wd_ref,
    out_ref, k_buf, v_buf, kn_buf, vn_buf,
    pos, freq, x_buf, gain, gain2, wq_buf, wo_buf, wg_buf, wd_buf,
    r_buf, q_buf, part, part_rx, o_buf, ob_buf, rs_tx, rs_rx, ag_buf, ss_buf, r2_buf,
    act_buf, dn_buf, rs2_tx, rs2_rx, ag2_buf,
    in_sem, wq_sem, k_sem, v_sem, wo_sem, wg_sem, wd_sem,
    a_sem, b_sem, s_sem, g_sem, c_sem, d_sem, e_sem,
):
    dp, t, s = lax.axis_index("dp"), lax.axis_index("tp"), lax.axis_index("sp")
    rows, dim = x_ref.shape
    keys = k_ref.shape[1]
    units = wg_buf.shape[1] // 2
    ffn = wd_ref.shape[0]
    depth = dim // W_CHUNKS

    def peer(off):
        return (dp, t ^ off[0], s ^ off[1])

    def piece_of(off):
        return (s ^ off[1] ^ 1) * TP + (t ^ off[0])

    me = piece_of((0, 0))

    def remote(src, dst, sems, k, off):
        return pltpu.make_async_remote_copy(
            src_ref=src, dst_ref=dst, send_sem=sems.at[0, k], recv_sem=sems.at[1, k],
            device_id=peer(off), device_id_type=MESH,
        )

    small = [
        pltpu.make_async_copy(src, dst, in_sem.at[i])
        for i, (src, dst) in enumerate((
            (x_ref, x_buf), (gain_ref, gain), (freq_ref, freq), (pos_ref, pos), (gain2_ref, gain2)
        ))
    ]
    for copy in small:
        copy.start()

    def wq_copy(c):
        return pltpu.make_async_copy(wq_ref.at[pl.ds(c * depth, depth)], wq_buf.at[c], wq_sem.at[c])

    def k_copy(b):
        return pltpu.make_async_copy(k_ref.at[b], k_buf.at[b], k_sem.at[b])

    def v_copy(b):
        return pltpu.make_async_copy(v_ref.at[b], v_buf.at[b], v_sem.at[b])

    def wo_copy(d):
        col = pl.multiple_of((s * TP + d) * 256, 256)
        return pltpu.make_async_copy(wo_ref.at[:, pl.ds(col, 256)], wo_buf.at[d], wo_sem.at[d])

    def wg_copy(c, half):
        col = pl.multiple_of(half * ffn + s * units, 128)
        return pltpu.make_async_copy(
            wg_ref.at[pl.ds(c * 512, 512), pl.ds(col, units)],
            wg_buf.at[pl.ds(c * 512, 512), pl.ds(half * units, units)],
            wg_sem.at[c, half],
        )

    def wd_copy(c):
        col = pl.multiple_of(s * 1024, 1024)
        return pltpu.make_async_copy(
            wd_ref.at[pl.ds(c * units, units), pl.ds(col, 1024)], wd_buf.at[c], wd_sem.at[c]
        )

    def start_kv(b):
        k_copy(b).start()
        v_copy(b).start()

    for c in range(W_CHUNKS):
        wq_copy(c).start()
    for b in range(AHEAD):
        start_kv(b)
    barrier = pltpu.get_barrier_semaphore()
    for off in OFFSETS:
        pl.semaphore_signal(barrier, inc=1, device_id=peer(off), device_id_type=MESH)

    small[0].wait()
    small[1].wait()
    x = x_buf[...].astype(F32)
    scale = lax.rsqrt(jnp.mean(x * x, axis=-1, keepdims=True) + NORM_EPS)
    r_buf[...] = (x * scale * gain[...]).astype(BF16)
    small[2].wait()
    small[3].wait()
    row_id = lax.broadcasted_iota(jnp.int32, (rows, 128), 0)
    lane_id = lax.broadcasted_iota(jnp.int32, (rows, 128), 1)
    diag = row_id == lane_id

    qkv = None
    for c in range(W_CHUNKS):
        wq_copy(c).wait()
        for b in range(AHEAD + c, rows if c == W_CHUNKS - 1 else AHEAD + c + 1):
            start_kv(b)
        term = jnp.dot(r_buf[:, c * depth:(c + 1) * depth], wq_buf[c], preferred_element_type=F32)
        qkv = term if qkv is None else qkv + term
        if c == 1:
            pos_col = jnp.zeros((rows, 128), jnp.int32)
            for b in range(rows):
                pos_col = jnp.where(row_id == b, pos[b], pos_col)
            angle = pos_col.astype(F32) * freq[...]
            cos = jnp.cos(angle)
            sin = jnp.sin(angle)
            sin = jnp.where(lane_id < 64, -sin, sin)

    def rotate(vals):
        out = vals * cos + pltpu.roll(vals, 64, 1) * sin
        return out.astype(BF16).astype(F32)

    for kv in range(2):
        base = kv * 768
        for h in range(4):
            q_buf[:, kv * 4 + h, :] = rotate(qkv[:, base + h * 128:base + (h + 1) * 128])
        kn_buf[kv] = rotate(qkv[:, base + 512:base + 640])
        vn_buf[kv] = qkv[:, base + 640:base + 768].astype(BF16).astype(F32)

    pl.semaphore_wait(barrier, len(OFFSETS))
    first_slot = s * (keys // 2)
    lane = lax.broadcasted_iota(jnp.int32, (8, keys), 1)
    head = lax.broadcasted_iota(jnp.int32, (8, keys), 0)
    own = (lane & 1) == (head >> 2)
    slot_id = lane >> 1
    lane8 = lax.broadcasted_iota(jnp.int32, (8, 128), 1)
    sub8 = lax.broadcasted_iota(jnp.int32, (8, 128), 0)
    low_heads = sub8 < 4
    scale = 128 ** -0.5

    def new_rows(buf, b):
        return jnp.where(low_heads, buf[0, pl.ds(b, 1), :], buf[1, pl.ds(b, 1), :])

    def a_rows(g):
        return pl.ds(g * GROUP, GROUP + (2 if g == rows // GROUP - 1 else 0))

    def a_copy(g, k, off):
        return remote(part.at[a_rows(g)], part_rx.at[k, a_rows(g)], a_sem.at[g], k, off)

    def a_forward(g):
        return remote(part_rx.at[2, a_rows(g)], part_rx.at[1, a_rows(g)], a_sem.at[g], 1, (0, 1))

    a_sends = []
    m_all = jnp.zeros((8, 128), F32)
    l_all = jnp.zeros((8, 128), F32)
    n_all = jnp.zeros((8, 128), F32)
    for g in range(rows // GROUP):
        ids = range(g * GROUP, (g + 1) * GROUP)
        scores = []
        for b in ids:
            k_copy(b).wait()
            q = q_buf[b]
            scores.append(lax.dot_general(
                q.astype(BF16), k_buf[b], (((1,), (1,)), ((), ())), preferred_element_type=F32
            ))
            fresh = jnp.sum(q * new_rows(kn_buf, b), axis=-1, keepdims=True) * scale
            n_all = jnp.where(lane8 == sub8 + b * 8, fresh, n_all)
        probs = []
        for b, sc in zip(ids, scores):
            ploc = pos[b] - first_slot
            mask = own & (slot_id < ploc) & (slot_id >= ploc - WINDOW)
            sc = jnp.where(mask, sc * scale, NEG)
            m = jnp.max(sc, axis=-1, keepdims=True)
            w = jnp.where(mask, jnp.exp(sc - m), 0.0)
            l = jnp.sum(w, axis=-1, keepdims=True)
            at = lane8 == sub8 + b * 8
            m_all = jnp.where(at, m, m_all)
            l_all = jnp.where(at, l, l_all)
            probs.append(w.astype(BF16))
        for b, w in zip(ids, probs):
            v_copy(b).wait()
            part[b] = jnp.dot(w, v_buf[b], preferred_element_type=F32)
        if g == rows // GROUP - 1:
            part[rows] = m_all
            part[rows + 1] = l_all
        for k, off in ((2, (0, 3)), (0, (0, 1))):
            copy = a_copy(g, k, off)
            copy.start()
            a_sends.append(copy)
        if g == 1:
            for d in range(TP):
                wo_copy(d).start()
        if g >= 2:
            for c in range((g - 2) * 4, (g - 1) * 4):
                wg_copy(c, 0).start()
                wg_copy(c, 1).start()
    for c in range(SP):
        wd_copy(c).start()

    for g in range(rows // GROUP):
        a_copy(g, 2, (0, 3)).wait_recv()
        copy = a_forward(g)
        copy.start()
        a_sends.append(copy)
    for g in range(rows // GROUP):
        a_copy(g, 0, (0, 1)).wait_recv()
        a_copy(g, 1, (0, 1)).wait_recv()
    parts = [part, part_rx.at[0], part_rx.at[1], part_rx.at[2]]
    top = n_all
    for p in parts:
        top = jnp.maximum(top, p[rows])
    facs = [jnp.exp(p[rows] - top) for p in parts]
    fresh = jnp.exp(n_all - top)
    total = fresh
    for p, f in zip(parts, facs):
        total = total + p[rows + 1] * f
    inv = 1.0 / total
    facs = [f * inv for f in facs]
    fresh = fresh * inv
    for b in range(rows):
        at = lane8 == sub8 + b * 8
        o = new_rows(vn_buf, b) * jnp.sum(jnp.where(at, fresh, 0.0), axis=-1, keepdims=True)
        for p, f in zip(parts, facs):
            o = o + p[b] * jnp.sum(jnp.where(at, f, 0.0), axis=-1, keepdims=True)
        o_buf[b] = o
    for h in range(8):
        ob_buf[:, h * 128:(h + 1) * 128] = o_buf[:, h, :].astype(BF16)

    def reduce_scatter(make_term, tx, rx, sems):
        sends = []
        for dt in (3, 2, 1, 0):
            tx[dt] = make_term(t ^ dt)
            copy = remote(tx.at[dt], rx.at[dt], sems, dt, (dt, 1))
            copy.start()
            sends.append(copy)
        for copy in sends:
            copy.wait()
        return rx[0] + rx[1] + rx[2] + rx[3]

    small[4].wait()
    for d in range(TP):
        wo_copy(d).wait()
    o_all = ob_buf[...]

    def out_term(d):
        return jnp.dot(o_all, wo_buf[d], preferred_element_type=F32).astype(BF16).astype(F32)

    my_cols = pl.ds(pl.multiple_of(me * 256, 256), 256)
    mid = x_buf[:, my_cols].astype(F32) + reduce_scatter(out_term, rs_tx, rs_rx, b_sem)
    ag_buf[me] = mid
    sq = jnp.sum(mid * mid, axis=-1, keepdims=True)
    ss_buf[me] = jnp.sum(jnp.where(diag, sq, 0.0), axis=0, keepdims=True)

    class Gather:
        def __init__(self, buf, sems):
            self.buf, self.sems, self.sends = buf, sems, []

        def send(self, have):
            for k in reversed(range(len(OFFSETS))):
                off = OFFSETS[k]
                if add_offsets(off, VIA[off]) == have:
                    slot = piece_of(have)
                    copy = remote(self.buf.at[slot], self.buf.at[slot], self.sems, k, VIA[off])
                    copy.start()
                    self.sends.append(copy)

        def wait(self, off):
            slot = piece_of(off)
            k = OFFSETS.index(off)
            remote(self.buf.at[slot], self.buf.at[slot], self.sems, k, VIA[off]).wait_recv()
            self.send(off)

    ss_sends = []
    for k in sorted(range(len(OFFSETS)), key=lambda i: -OFFSETS[i][0]):
        copy = remote(ss_buf.at[me], ss_buf.at[me], s_sem, k, OFFSETS[k])
        copy.start()
        ss_sends.append(copy)
    gather = Gather(ag_buf, g_sem)
    gather.send((0, 0))
    for off in OFFSETS[:6]:
        gather.wait(off)
    for k in range(len(OFFSETS)):
        slot = piece_of(OFFSETS[k])
        remote(ss_buf.at[slot], ss_buf.at[slot], s_sem, k, OFFSETS[k]).wait_recv()
    tot = jnp.sum(ss_buf[...], axis=0)
    mean_sq = jnp.sum(jnp.where(diag, tot, 0.0), axis=-1, keepdims=True) / dim
    rstd = lax.rsqrt(mean_sq + NORM_EPS)
    for c in range(8):
        wg_copy(c, 0).wait()
        wg_copy(c, 1).wait()

    def gate_up(ds):
        block = s ^ ds ^ 1
        for j in range(TP):
            at = pl.ds(pl.multiple_of((block * TP + j) * 256, 256), 256)
            r2_buf[ds, :, j * 256:(j + 1) * 256] = (ag_buf[block * TP + j] * rstd * gain2[:, at]).astype(BF16)
        at = pl.ds(pl.multiple_of(block * 1024, 1024), 1024)
        return jnp.dot(r2_buf[ds], wg_buf[at, :], preferred_element_type=F32)

    hid = gate_up(1)
    for off in OFFSETS[6:8] + OFFSETS[8:9]:
        gather.wait(off)
    for off in ((1, 0), (2, 0), (3, 0)):
        gather.wait(off)
    hid = hid + gate_up(0) + gate_up(3)
    for off in ((1, 2), (2, 2), (3, 2)):
        gather.wait(off)
    hid = hid + gate_up(2)
    gate, up = hid[:, :units], hid[:, units:]
    act_buf[s] = (gate * jax.nn.sigmoid(gate) * up).astype(BF16).astype(F32)

    act_sends = []

    def act_send(slot, k, off):
        copy = remote(act_buf.at[slot], act_buf.at[slot], c_sem, k, off)
        copy.start()
        act_sends.append(copy)

    act_send(s, 2, (0, 3))
    act_send(s, 0, (0, 1))
    for c in range(SP):
        wd_copy(c).wait()
    down = jnp.dot(act_buf[s].astype(BF16), wd_buf[s], preferred_element_type=F32)
    for k in (0, 2, 1):
        slot = s ^ (k + 1)
        remote(act_buf.at[slot], act_buf.at[slot], c_sem, k, (0, 1)).wait_recv()
        if k == 2:
            act_send(slot, 1, (0, 1))
        down = down + jnp.dot(act_buf[slot].astype(BF16), wd_buf[slot], preferred_element_type=F32)
    down = down.astype(BF16).astype(F32)
    for d in range(TP):
        dn_buf[d] = down[:, d * 256:(d + 1) * 256]

    def down_term(d):
        return dn_buf[d]

    ag2_buf[me] = mid + reduce_scatter(down_term, rs2_tx, rs2_rx, d_sem)
    gather2 = Gather(ag2_buf, e_sem)
    gather2.send((0, 0))
    for off in OFFSETS:
        gather2.wait(off)
    for i in range(16):
        out_ref[:, i * 256:(i + 1) * 256] = ag2_buf[i]
    for copy in a_sends + ss_sends + gather.sends + act_sends + gather2.sends:
        copy.wait_send()


def store_kernel(
    pos_ref, x2_ref, kn_ref, vn_ref, k_in, v_in, out_ref, k_out, v_out, k_buf, v_buf,
    pos, x2, pos_sem, x_sem, k_sem, v_sem,
):
    rows, keys = k_out.shape[:2]
    load = pltpu.make_async_copy(pos_ref, pos, pos_sem)
    load.start()
    x2[...] = x2_ref[...].astype(BF16)
    out = pltpu.make_async_copy(x2, out_ref, x_sem)
    out.start()
    load.wait()
    first_slot = lax.axis_index("sp") * (keys // 2)
    row16 = lax.broadcasted_iota(jnp.int32, (16, 128), 0)

    def put(ref, new, b, ploc):
        start = pl.multiple_of((jnp.clip(ploc * 2, 0, keys - 2) // 16) * 16, 16)
        block = ref[b, pl.ds(start, 16), :].astype(F32)
        at = row16 + start
        block = jnp.where(at == ploc * 2, new[0, b:b + 1, :], block)
        block = jnp.where(at == ploc * 2 + 1, new[1, b:b + 1, :], block)
        ref[b, pl.ds(start, 16), :] = block.astype(BF16)

    copies = [out]
    for b in range(rows):
        ploc = pos[b] - first_slot
        put(k_buf, kn_ref, b, ploc)
        copies.append(pltpu.make_async_copy(k_buf.at[b], k_out.at[b], k_sem.at[b]))
        copies[-1].start()
        put(v_buf, vn_ref, b, ploc)
        copies.append(pltpu.make_async_copy(v_buf.at[b], v_out.at[b], v_sem.at[b]))
        copies[-1].start()
    for copy in copies:
        copy.wait()


def solution(mesh):
    cache_spec = P("dp", "sp", "tp", None)
    vmem = pl.BlockSpec(memory_space=pltpu.VMEM)
    hbm = pl.BlockSpec(memory_space=pltpu.HBM)

    def in_hbm(*arrays):
        return tuple(pltpu.with_memory_space_constraint(a, pltpu.HBM) for a in arrays)

    def local_step(hidden, positions, norm_attn, norm_mlp, w_qkv, w_out, w_gate_up, w_down, k_cache, v_cache):
        rows, block_len, kv_local, head_dim = k_cache.shape
        dim = hidden.shape[1]
        flat = (rows, block_len * kv_local, head_dim)
        freq = ROPE_BASE ** (-np.arange(0, head_dim, 2, dtype=np.float64) / head_dim)
        freq = jnp.asarray(np.concatenate([freq, freq])[None].astype(np.float32))
        units = w_down.shape[0] // SP
        fresh = (kv_local, rows, head_dim)
        x2, k_mid, v_mid, k_new, v_new = pl.pallas_call(
            layer_kernel,
            out_shape=(
                pltpu.VMEM((rows, dim), F32),
                pltpu.VMEM(flat, BF16),
                pltpu.VMEM(flat, BF16),
                pltpu.VMEM(fresh, F32),
                pltpu.VMEM(fresh, F32),
            ),
            in_specs=[hbm] * 11,
            out_specs=(vmem,) * 5,
            scratch_shapes=[
                pltpu.SMEM((rows,), jnp.int32),
                pltpu.VMEM((1, head_dim), F32),
                pltpu.VMEM((rows, dim), BF16),
                pltpu.VMEM((1, dim), F32),
                pltpu.VMEM((1, dim), F32),
                pltpu.VMEM((W_CHUNKS, dim // W_CHUNKS, w_qkv.shape[1]), BF16),
                pltpu.VMEM((TP, 1024, 256), BF16),
                pltpu.VMEM((dim, 2 * units), BF16),
                pltpu.VMEM((SP, units, 1024), BF16),
                pltpu.VMEM((rows, dim), BF16),
                pltpu.VMEM((rows, 8, 128), F32),
                pltpu.VMEM((rows + 2, 8, 128), F32),
                pltpu.VMEM((3, rows + 2, 8, 128), F32),
                pltpu.VMEM((rows, 8, 128), F32),
                pltpu.VMEM((rows, 1024), BF16),
                pltpu.VMEM((TP, rows, 256), F32),
                pltpu.VMEM((TP, rows, 256), F32),
                pltpu.VMEM((16, rows, 256), F32),
                pltpu.VMEM((16, 1, 128), F32),
                pltpu.VMEM((SP, rows, 1024), BF16),
                pltpu.VMEM((SP, rows, units), F32),
                pltpu.VMEM((TP, rows, 256), F32),
                pltpu.VMEM((TP, rows, 256), F32),
                pltpu.VMEM((TP, rows, 256), F32),
                pltpu.VMEM((16, rows, 256), F32),
                pltpu.SemaphoreType.DMA((5,)),
                pltpu.SemaphoreType.DMA((W_CHUNKS,)),
                pltpu.SemaphoreType.DMA((rows,)),
                pltpu.SemaphoreType.DMA((rows,)),
                pltpu.SemaphoreType.DMA((TP,)),
                pltpu.SemaphoreType.DMA((8, 2)),
                pltpu.SemaphoreType.DMA((SP,)),
                pltpu.SemaphoreType.DMA((rows // GROUP, 2, 3)),
                pltpu.SemaphoreType.DMA((2, 4)),
                pltpu.SemaphoreType.DMA((2, 15)),
                pltpu.SemaphoreType.DMA((2, 15)),
                pltpu.SemaphoreType.DMA((2, 3)),
                pltpu.SemaphoreType.DMA((2, 4)),
                pltpu.SemaphoreType.DMA((2, 15)),
            ],
            compiler_params=pltpu.CompilerParams(
                collective_id=0, has_side_effects=True, vmem_limit_bytes=44 * 2 ** 20
            ),
            cost_estimate=pl.CostEstimate(flops=4 * 10 ** 9, bytes_accessed=6 * 10 ** 7, transcendentals=10 ** 6),
        )(*in_hbm(
            positions, freq, hidden, norm_attn.reshape(1, dim), norm_mlp.reshape(1, dim), w_qkv,
            k_cache.reshape(flat), v_cache.reshape(flat), w_out, w_gate_up, w_down,
        ))
        result, k_upd, v_upd, _, _ = pl.pallas_call(
            store_kernel,
            out_shape=(
                jax.ShapeDtypeStruct((rows, dim), BF16),
                jax.ShapeDtypeStruct(flat, BF16),
                jax.ShapeDtypeStruct(flat, BF16),
                pltpu.VMEM(flat, BF16),
                pltpu.VMEM(flat, BF16),
            ),
            in_specs=[hbm] + [vmem] * 5,
            out_specs=(hbm, hbm, hbm, vmem, vmem),
            input_output_aliases={4: 3, 5: 4},
            scratch_shapes=[
                pltpu.SMEM((rows,), jnp.int32),
                pltpu.VMEM((rows, dim), BF16),
                pltpu.SemaphoreType.DMA,
                pltpu.SemaphoreType.DMA,
                pltpu.SemaphoreType.DMA((rows,)),
                pltpu.SemaphoreType.DMA((rows,)),
            ],
            compiler_params=pltpu.CompilerParams(vmem_limit_bytes=8 * 2 ** 20),
            cost_estimate=pl.CostEstimate(flops=10 ** 8, bytes_accessed=2 * 10 ** 7, transcendentals=0),
        )(*in_hbm(positions), x2, k_new, v_new, k_mid, v_mid)
        return result, k_upd.reshape(k_cache.shape), v_upd.reshape(v_cache.shape)

    return jax.shard_map(
        local_step, mesh=mesh,
        in_specs=(P("dp", None), P("dp"), P(None), P(None), P(None, "tp"), P("tp", None), P(None, "tp"), P("tp", None), cache_spec, cache_spec),
        out_specs=(P("dp", None), cache_spec, cache_spec), check_vma=False,
    )
```

time: 217 us -> 56.7 us (0.26)
  waiting for transfers between devices: 92.1 us -> 0 us
  Pallas kernels: 0 us -> 55.9 us
  matrix products: 52.5 us -> 0 us
  other arithmetic: 31.8 us -> 0 us
  blocking collectives: 22.9 us -> 0 us
  between operations: 13.9 us -> 0.64 us
  local copies, waits for them, and re-layouts: 3.51 us -> 0 us
    psum x3 -> x0, waiting for transfers between devices: 92.1 us -> none  [the longest x1 35.4 us: layer_tail(): result = mid_resid + lax.psum(down_part, 'tp')]
    pallas_call x0 -> x2, Pallas kernels: none -> 55.9 us  [the longest x1 49.1 us: local_step(): pl.pallas_call(layer_kernel, out_shape=(pltpu.VMEM((rows, dim), F32), plt...]
    dot_general x6 -> x0, matrix products: 52.5 us -> none  [the longest x1 20.8 us: layer_tail(): gate_up = jnp.dot(normed_mlp, w_gate_up, preferred_element_type=jnp.float32)]
    select_n x1 -> x0, other arithmetic: 26.2 us -> none  [write_entry(): return jnp.where(at_slot, entry[:, None], cache)]
    pmax x1 -> x0, blocking collectives: 12.7 us -> none  [window_attention(): glob_max = lax.pmax(jnp.max(scores, axis=-1), 'sp')]
    psum x1 -> x0, blocking collectives: 10.1 us -> none  [window_attention(): weight_sum = lax.psum(jnp.sum(weights, axis=-1), 'sp')]
    unnamed x10 -> x0, local copies, waits for them, and re-layouts: 3.41 us -> none
    convert_element_type x3 -> x0, other arithmetic: 2.68 us -> none  [the longest x1 1.64 us: layer_tail(): return result.astype(jnp.bfloat16)]
  transfers between devices with their start and end apart: 3 -> 0, of which waited for: 3 -> 0; matrix products, arithmetic and copies ran while one was open for 0% -> 0% of each run, Pallas kernels for 0% -> 0%
where the time goes in v3:
time: 56.7 us; the launch traced here: 56.6 us
  Pallas kernels  55.9 us (99%)
  between operations  0.64 us (1%)
    pallas_call x1, Pallas kernels, local_step(): pl.pallas_call(layer_kernel, out_shape=(pltpu.VMEM((rows, dim), F32), plt...  49.1 us
    pallas_call x1, Pallas kernels, local_step(): pl.pallas_call(store_kernel, out_shape=(jax.ShapeDtypeStruct((rows, dim),...  6.78 us

profile of v3, /device:TPU:0, one launch (start us, length us, event | category | flops | bytes accessed | tf_op | source)
XLA Modules:
  0.0 56.6 jit_solution(7199293743436959710)
XLA Ops:
  0.6 49.1 %shard_map.130 = (f32[16,4096]{1,0:T(8,128)S(1)}, bf16[16,2048,128]{2,1,0:T(8,128)(2,1)S(1)}, bf16[16,2048,128]{2,1,0:T(8,128)(2,1)S(1)}, f32[2,16,128]{2,1,0:T(8,128)S(1)}, f32[2,16,128]{2,1,0:T(8,128)S(1)}) custom-call(s32[16]{0:T(128)} %pos_ref.3, f32[1,128]{1,0:T(1,128)} %constant.2.clone.freq_ref, bf16[16,4096]{1,0:T(8,128)(2,1)} %x_ref.1, ...), custom_call_target="tpu_custom_call" | custom-call | flops 4000000000 | bytes 60000000 | tf_op jit(solution)/shard_map/pallas_call | solution.py:418
  49.8 6.8 %shard_map.131 = (bf16[16,4096]{1,0:T(8,128)(2,1)}, bf16[16,2048,128]{2,1,0:T(8,128)(2,1)}, bf16[16,2048,128]{2,1,0:T(8,128)(2,1)}, bf16[16,2048,128]{2,1,0:T(8,128)(2,1)S(1)}, bf16[16,2048,128]{2,1,0:T(8,128)(2,1)S(1)}) custom-call(s32[16]{0:T(128)} %pos_ref.3, ...), custom_call_target="tpu_custom_call", output_to_operand_aliasing={{3}: (4, {}), {4}: (5, {})} | custom-call | flops 100000000 | bytes 20000000 | tf_op jit(solution)/shard_map/pallas_call | solution.py:478

commit v4 on v3

v4 whole, which is shorter than its diff:
```python
import jax
import jax.numpy as jnp
import numpy as np
from jax import lax
from jax.experimental import pallas as pl
from jax.experimental.pallas import tpu as pltpu
from jax.sharding import PartitionSpec as P

WINDOW = 2047
ROPE_BASE = 10000.0
NORM_EPS = 1e-5
MESH = pl.DeviceIdType.MESH
F32 = jnp.float32
BF16 = jnp.bfloat16
NEG = float(jnp.finfo(jnp.float32).min)

TP = 4
SP = 4
W_CHUNKS = 8
GROUP = 4
OFFSETS = (
    (0, 1), (0, 3), (1, 1), (2, 1), (1, 3), (3, 1), (2, 3), (3, 3),
    (0, 2), (1, 0), (2, 0), (1, 2), (3, 0), (2, 2), (3, 2),
)
VIA = {off: off if off[1] & 1 else (0, 1) for off in OFFSETS}


def add_offsets(a, b):
    return (a[0] ^ b[0], a[1] ^ b[1])


def layer_kernel(
    pos_ref, freq_ref, x_ref, gain_ref, gain2_ref, wq_ref, k_ref, v_ref, wo_ref, wg_ref, wd_ref,
    out_ref, k_buf, v_buf, kn_buf, vn_buf, pos,
    freq, x_buf, gain, gain2, wq_buf, wo_buf, wg_buf, wd_buf,
    r_buf, q_buf, part, part_rx, o_buf, ob_buf, rs_tx, rs_rx, ag_buf, ss_buf, r2_buf,
    act_buf, dn_buf, rs2_tx, rs2_rx, ag2_buf,
    in_sem, wq_sem, k_sem, v_sem, wo_sem, wg_sem, wd_sem,
    a_sem, b_sem, s_sem, g_sem, c_sem, d_sem, e_sem, send_sem,
):
    dp, t, s = lax.axis_index("dp"), lax.axis_index("tp"), lax.axis_index("sp")
    rows, dim = x_ref.shape
    keys = k_ref.shape[1]
    units = wg_buf.shape[1] // 2
    ffn = wd_ref.shape[0]
    depth = dim // W_CHUNKS

    def peer(off):
        return (dp, t ^ off[0], s ^ off[1])

    def piece_of(off):
        return (s ^ off[1] ^ 1) * TP + (t ^ off[0])

    me = piece_of((0, 0))

    def remote(src, dst, phase, recv, off):
        return pltpu.make_async_remote_copy(
            src_ref=src, dst_ref=dst, send_sem=send_sem.at[phase], recv_sem=recv,
            device_id=peer(off), device_id_type=MESH,
        )

    def wait_bytes(ref, sem):
        pltpu.make_async_copy(ref, ref, sem).wait()

    small = [
        pltpu.make_async_copy(src, dst, in_sem.at[i])
        for i, (src, dst) in enumerate((
            (x_ref, x_buf), (gain_ref, gain), (freq_ref, freq), (pos_ref, pos), (gain2_ref, gain2)
        ))
    ]
    for copy in small:
        copy.start()

    def wq_copy(c):
        return pltpu.make_async_copy(wq_ref.at[pl.ds(c * depth, depth)], wq_buf.at[c], wq_sem.at[c])

    def k_copy(g):
        at = pl.ds(g * GROUP, GROUP)
        return pltpu.make_async_copy(k_ref.at[at], k_buf.at[at], k_sem.at[g])

    def v_copy(g):
        at = pl.ds(g * GROUP, GROUP)
        return pltpu.make_async_copy(v_ref.at[at], v_buf.at[at], v_sem.at[g])

    def start_wo():
        for d in range(TP):
            col = pl.multiple_of((s * TP + d) * 256, 256)
            pltpu.make_async_copy(wo_ref.at[:, pl.ds(col, 256)], wo_buf.at[d], wo_sem).start()

    def start_wg(c):
        for half in range(2):
            col = pl.multiple_of(half * ffn + s * units, 128)
            pltpu.make_async_copy(
                wg_ref.at[pl.ds(c * 1024, 1024), pl.ds(col, units)],
                wg_buf.at[pl.ds(c * 1024, 1024), pl.ds(half * units, units)],
                wg_sem,
            ).start()

    def start_wd():
        for c in range(SP):
            col = pl.multiple_of(s * 1024, 1024)
            pltpu.make_async_copy(
                wd_ref.at[pl.ds(c * units, units), pl.ds(col, 1024)], wd_buf.at[c], wd_sem
            ).start()

    wq_copy(0).start()
    wq_copy(1).start()
    barrier = pltpu.get_barrier_semaphore()
    for off in OFFSETS:
        pl.semaphore_signal(barrier, inc=1, device_id=peer(off), device_id_type=MESH)

    for copy in small:
        copy.wait()
    for c in range(2, W_CHUNKS):
        wq_copy(c).start()
    x = x_buf[...].astype(F32)
    scale = lax.rsqrt(jnp.mean(x * x, axis=-1, keepdims=True) + NORM_EPS)
    r_buf[...] = (x * scale * gain[...]).astype(BF16)
    row_id = lax.broadcasted_iota(jnp.int32, (rows, 128), 0)
    lane_id = lax.broadcasted_iota(jnp.int32, (rows, 128), 1)
    diag = row_id == lane_id

    qkv = None
    for c in range(W_CHUNKS):
        wq_copy(c).wait()
        if c >= W_CHUNKS - GROUP:
            k_copy(c - W_CHUNKS + GROUP).start()
            v_copy(c - W_CHUNKS + GROUP).start()
        term = jnp.dot(r_buf[:, c * depth:(c + 1) * depth], wq_buf[c], preferred_element_type=F32)
        qkv = term if qkv is None else qkv + term
        if c == 1:
            pos_col = jnp.zeros((rows, 128), jnp.int32)
            for b in range(rows):
                pos_col = jnp.where(row_id == b, pos[b], pos_col)
            angle = pos_col.astype(F32) * freq[...]
            cos = jnp.cos(angle)
            sin = jnp.sin(angle)
            sin = jnp.where(lane_id < 64, -sin, sin)

    def rotate(vals):
        out = vals * cos + pltpu.roll(vals, 64, 1) * sin
        return out.astype(BF16).astype(F32)

    for kv in range(2):
        base = kv * 768
        for h in range(4):
            q_buf[:, kv * 4 + h, :] = rotate(qkv[:, base + h * 128:base + (h + 1) * 128])
        kn_buf[kv] = rotate(qkv[:, base + 512:base + 640])
        vn_buf[kv] = qkv[:, base + 640:base + 768].astype(BF16).astype(F32)

    pl.semaphore_wait(barrier, len(OFFSETS))
    first_slot = s * (keys // 2)
    lane = lax.broadcasted_iota(jnp.int32, (8, keys), 1)
    head = lax.broadcasted_iota(jnp.int32, (8, keys), 0)
    own = (lane & 1) == (head >> 2)
    slot_id = lane >> 1
    lane8 = lax.broadcasted_iota(jnp.int32, (8, 128), 1)
    sub8 = lax.broadcasted_iota(jnp.int32, (8, 128), 0)
    low_heads = sub8 < 4
    scale = 128 ** -0.5

    def new_rows(buf, b):
        return jnp.where(low_heads, buf[0, pl.ds(b, 1), :], buf[1, pl.ds(b, 1), :])

    def a_rows(g):
        return pl.ds(g * GROUP, GROUP + (2 if g == rows // GROUP - 1 else 0))

    groups = rows // GROUP

    def a_copy(g, k, off):
        recv = a_sem.at[g if k == 2 else groups]
        return remote(part.at[a_rows(g)], part_rx.at[k, a_rows(g)], 0, recv, off)

    def a_forward(g):
        return remote(part_rx.at[2, a_rows(g)], part_rx.at[1, a_rows(g)], 0, a_sem.at[groups + 1], (0, 1))

    m_all = jnp.zeros((8, 128), F32)
    l_all = jnp.zeros((8, 128), F32)
    n_all = jnp.zeros((8, 128), F32)
    for g in range(rows // GROUP):
        ids = range(g * GROUP, (g + 1) * GROUP)
        k_copy(g).wait()
        v_copy(g).wait()
        scores = []
        for b in ids:
            q = q_buf[b]
            scores.append(lax.dot_general(
                q.astype(BF16), k_buf[b], (((1,), (1,)), ((), ())), preferred_element_type=F32
            ))
            fresh = jnp.sum(q * new_rows(kn_buf, b), axis=-1, keepdims=True) * scale
            n_all = jnp.where(lane8 == sub8 + b * 8, fresh, n_all)
        probs = []
        for b, sc in zip(ids, scores):
            ploc = pos[b] - first_slot
            mask = own & (slot_id < ploc) & (slot_id >= ploc - WINDOW)
            sc = jnp.where(mask, sc * scale, NEG)
            m = jnp.max(sc, axis=-1, keepdims=True)
            w = jnp.where(mask, jnp.exp(sc - m), 0.0)
            l = jnp.sum(w, axis=-1, keepdims=True)
            at = lane8 == sub8 + b * 8
            m_all = jnp.where(at, m, m_all)
            l_all = jnp.where(at, l, l_all)
            probs.append(w.astype(BF16))
        for b, w in zip(ids, probs):
            part[b] = jnp.dot(w, v_buf[b], preferred_element_type=F32)
        if g == rows // GROUP - 1:
            part[rows] = m_all
            part[rows + 1] = l_all
        for k, off in ((2, (0, 3)), (0, (0, 1))):
            a_copy(g, k, off).start()
        if g == 1:
            start_wo()
        if g == 2:
            start_wg(0)
            start_wg(1)
        if g == 3:
            start_wg(2)
            start_wg(3)
            start_wd()

    for g in range(rows // GROUP):
        a_copy(g, 2, (0, 3)).wait_recv()
        a_forward(g).start()
    wait_bytes(part_rx.at[0], a_sem.at[groups])
    wait_bytes(part_rx.at[1], a_sem.at[groups + 1])
    parts = [part, part_rx.at[0], part_rx.at[1], part_rx.at[2]]
    top = n_all
    for p in parts:
        top = jnp.maximum(top, p[rows])
    facs = [jnp.exp(p[rows] - top) for p in parts]
    fresh = jnp.exp(n_all - top)
    total = fresh
    for p, f in zip(parts, facs):
        total = total + p[rows + 1] * f
    inv = 1.0 / total
    facs = [f * inv for f in facs]
    fresh = fresh * inv
    for b in range(rows):
        at = lane8 == sub8 + b * 8
        o = new_rows(vn_buf, b) * jnp.sum(jnp.where(at, fresh, 0.0), axis=-1, keepdims=True)
        for p, f in zip(parts, facs):
            o = o + p[b] * jnp.sum(jnp.where(at, f, 0.0), axis=-1, keepdims=True)
        o_buf[b] = o
    for h in range(8):
        ob_buf[:, h * 128:(h + 1) * 128] = o_buf[:, h, :].astype(BF16)

    def reduce_scatter(make_term, tx, rx, phase, sem):
        for dt in (3, 2, 1, 0):
            tx[dt] = make_term(t ^ dt)
            remote(tx.at[dt], rx.at[dt], phase, sem, (dt, 1)).start()
        wait_bytes(rx, sem)
        return rx[0] + rx[1] + rx[2] + rx[3]

    wait_bytes(wo_buf, wo_sem)
    o_all = ob_buf[...]

    def out_term(d):
        return jnp.dot(o_all, wo_buf[d], preferred_element_type=F32).astype(BF16).astype(F32)

    my_cols = pl.ds(pl.multiple_of(me * 256, 256), 256)
    mid = x_buf[:, my_cols].astype(F32) + reduce_scatter(out_term, rs_tx, rs_rx, 1, b_sem)
    ag_buf[me] = mid
    sq = jnp.sum(mid * mid, axis=-1, keepdims=True)
    ss_buf[me] = jnp.sum(jnp.where(diag, sq, 0.0), axis=0, keepdims=True)

    class Gather:
        def __init__(self, buf, sems, phase):
            self.buf, self.sems, self.phase = buf, sems, phase

        def send(self, have):
            for k in reversed(range(len(OFFSETS))):
                off = OFFSETS[k]
                if add_offsets(off, VIA[off]) == have:
                    slot = piece_of(have)
                    recv = self.sems.at[k if k < 8 else 8 + off[1] // 2]
                    remote(self.buf.at[slot], self.buf.at[slot], self.phase, recv, VIA[off]).start()

        def wait(self, off):
            slot = piece_of(off)
            k = OFFSETS.index(off)
            remote(self.buf.at[slot], self.buf.at[slot], self.phase, self.sems.at[k], off).wait_recv()
            self.send(off)

        def wait_block(self, ds):
            wait_bytes(self.buf.at[pl.ds(0, 3 if ds == 0 else 4)], self.sems.at[8 + ds // 2])

    for off in sorted(OFFSETS, key=lambda o: -o[0]):
        remote(ss_buf.at[me], ss_buf.at[me], 2, s_sem, off).start()
    gather = Gather(ag_buf, g_sem, 3)
    gather.send((0, 0))
    for off in OFFSETS[:8]:
        gather.wait(off)
    wait_bytes(ss_buf.at[pl.ds(0, len(OFFSETS))], s_sem)
    tot = jnp.sum(ss_buf[...], axis=0)
    mean_sq = jnp.sum(jnp.where(diag, tot, 0.0), axis=-1, keepdims=True) / dim
    rstd = lax.rsqrt(mean_sq + NORM_EPS)
    wait_bytes(wg_buf, wg_sem)

    def gate_up(ds):
        block = s ^ ds ^ 1
        for j in range(TP):
            at = pl.ds(pl.multiple_of((block * TP + j) * 256, 256), 256)
            r2_buf[ds, :, j * 256:(j + 1) * 256] = (ag_buf[block * TP + j] * rstd * gain2[:, at]).astype(BF16)
        at = pl.ds(pl.multiple_of(block * 1024, 1024), 1024)
        return jnp.dot(r2_buf[ds], wg_buf[at, :], preferred_element_type=F32)

    hid = gate_up(1) + gate_up(3)
    gather.wait_block(0)
    hid = hid + gate_up(0)
    gather.wait_block(2)
    hid = hid + gate_up(2)
    gate, up = hid[:, :units], hid[:, units:]
    act_buf[s] = (gate * jax.nn.sigmoid(gate) * up).astype(BF16).astype(F32)

    def act_send(slot, k, off):
        remote(act_buf.at[slot], act_buf.at[slot], 4, c_sem.at[k], off).start()

    act_send(s, 2, (0, 3))
    act_send(s, 0, (0, 1))
    wait_bytes(wd_buf, wd_sem)
    down = jnp.dot(act_buf[s].astype(BF16), wd_buf[s], preferred_element_type=F32)
    for k in (0, 2, 1):
        slot = s ^ (k + 1)
        remote(act_buf.at[slot], act_buf.at[slot], 4, c_sem.at[k], (0, 1)).wait_recv()
        if k == 2:
            act_send(slot, 1, (0, 1))
        down = down + jnp.dot(act_buf[slot].astype(BF16), wd_buf[slot], preferred_element_type=F32)
    down = down.astype(BF16).astype(F32)
    for d in range(TP):
        dn_buf[d] = down[:, d * 256:(d + 1) * 256]

    def down_term(d):
        return dn_buf[d]

    ag2_buf[me] = mid + reduce_scatter(down_term, rs2_tx, rs2_rx, 5, d_sem)
    gather2 = Gather(ag2_buf, e_sem, 6)
    gather2.send((0, 0))
    for off in OFFSETS[:8]:
        gather2.wait(off)
    gather2.wait_block(0)
    gather2.wait_block(2)
    for i in range(16):
        out_ref[:, i * 256:(i + 1) * 256] = ag2_buf[i]
    sent = (
        part_rx, rs_tx, ss_buf.at[pl.ds(0, 15)], ag_buf.at[pl.ds(0, 15)], act_buf.at[pl.ds(0, 3)],
        rs2_tx, ag2_buf.at[pl.ds(0, 15)],
    )
    for phase, ref in enumerate(sent):
        wait_bytes(ref, send_sem.at[phase])


def store_kernel(
    pos, x2_ref, kn_ref, vn_ref, k_in, v_in, out_ref, k_out, v_out, k_buf, v_buf, x2, x_sem, k_sem, v_sem
):
    rows, keys = k_out.shape[:2]
    x2[...] = x2_ref[...].astype(BF16)
    out = pltpu.make_async_copy(x2, out_ref, x_sem)
    out.start()
    first_slot = lax.axis_index("sp") * (keys // 2)
    row16 = lax.broadcasted_iota(jnp.int32, (16, 128), 0)

    def put(ref, new, b, ploc):
        start = pl.multiple_of((jnp.clip(ploc * 2, 0, keys - 2) // 16) * 16, 16)
        block = ref[b, pl.ds(start, 16), :].astype(F32)
        at = row16 + start
        block = jnp.where(at == ploc * 2, new[0, b:b + 1, :], block)
        block = jnp.where(at == ploc * 2 + 1, new[1, b:b + 1, :], block)
        ref[b, pl.ds(start, 16), :] = block.astype(BF16)

    for b in range(rows):
        ploc = pos[b] - first_slot
        put(k_buf, kn_ref, b, ploc)
        pltpu.make_async_copy(k_buf.at[b], k_out.at[b], k_sem).start()
        put(v_buf, vn_ref, b, ploc)
        pltpu.make_async_copy(v_buf.at[b], v_out.at[b], v_sem).start()
    out.wait()
    pltpu.make_async_copy(k_buf, k_out, k_sem).wait()
    pltpu.make_async_copy(v_buf, v_out, v_sem).wait()


def solution(mesh):
    cache_spec = P("dp", "sp", "tp", None)
    vmem = pl.BlockSpec(memory_space=pltpu.VMEM)
    smem = pl.BlockSpec(memory_space=pltpu.SMEM)
    hbm = pl.BlockSpec(memory_space=pltpu.HBM)

    def in_hbm(*arrays):
        return tuple(pltpu.with_memory_space_constraint(a, pltpu.HBM) for a in arrays)

    def local_step(hidden, positions, norm_attn, norm_mlp, w_qkv, w_out, w_gate_up, w_down, k_cache, v_cache):
        rows, block_len, kv_local, head_dim = k_cache.shape
        dim = hidden.shape[1]
        flat = (rows, block_len * kv_local, head_dim)
        freq = ROPE_BASE ** (-np.arange(0, head_dim, 2, dtype=np.float64) / head_dim)
        freq = jnp.asarray(np.concatenate([freq, freq])[None].astype(np.float32))
        units = w_down.shape[0] // SP
        fresh = (kv_local, rows, head_dim)
        x2, k_mid, v_mid, k_new, v_new, pos = pl.pallas_call(
            layer_kernel,
            out_shape=(
                pltpu.VMEM((rows, dim), F32),
                pltpu.VMEM(flat, BF16),
                pltpu.VMEM(flat, BF16),
                pltpu.VMEM(fresh, F32),
                pltpu.VMEM(fresh, F32),
                pltpu.SMEM((rows,), jnp.int32),
            ),
            in_specs=[hbm] * 11,
            out_specs=(vmem,) * 5 + (smem,),
            scratch_shapes=[
                pltpu.VMEM((1, head_dim), F32),
                pltpu.VMEM((rows, dim), BF16),
                pltpu.VMEM((1, dim), F32),
                pltpu.VMEM((1, dim), F32),
                pltpu.VMEM((W_CHUNKS, dim // W_CHUNKS, w_qkv.shape[1]), BF16),
                pltpu.VMEM((TP, 1024, 256), BF16),
                pltpu.VMEM((dim, 2 * units), BF16),
                pltpu.VMEM((SP, units, 1024), BF16),
                pltpu.VMEM((rows, dim), BF16),
                pltpu.VMEM((rows, 8, 128), F32),
                pltpu.VMEM((rows + 2, 8, 128), F32),
                pltpu.VMEM((3, rows + 2, 8, 128), F32),
                pltpu.VMEM((rows, 8, 128), F32),
                pltpu.VMEM((rows, 1024), BF16),
                pltpu.VMEM((TP, rows, 256), F32),
                pltpu.VMEM((TP, rows, 256), F32),
                pltpu.VMEM((16, rows, 256), F32),
                pltpu.VMEM((16, 1, 128), F32),
                pltpu.VMEM((SP, rows, 1024), BF16),
                pltpu.VMEM((SP, rows, units), F32),
                pltpu.VMEM((TP, rows, 256), F32),
                pltpu.VMEM((TP, rows, 256), F32),
                pltpu.VMEM((TP, rows, 256), F32),
                pltpu.VMEM((16, rows, 256), F32),
                pltpu.SemaphoreType.DMA((5,)),
                pltpu.SemaphoreType.DMA((W_CHUNKS,)),
                pltpu.SemaphoreType.DMA((rows // GROUP,)),
                pltpu.SemaphoreType.DMA((rows // GROUP,)),
                pltpu.SemaphoreType.DMA,
                pltpu.SemaphoreType.DMA,
                pltpu.SemaphoreType.DMA,
                pltpu.SemaphoreType.DMA((rows // GROUP + 2,)),
                pltpu.SemaphoreType.DMA,
                pltpu.SemaphoreType.DMA,
                pltpu.SemaphoreType.DMA((10,)),
                pltpu.SemaphoreType.DMA((3,)),
                pltpu.SemaphoreType.DMA,
                pltpu.SemaphoreType.DMA((10,)),
                pltpu.SemaphoreType.DMA((7,)),
            ],
            compiler_params=pltpu.CompilerParams(
                collective_id=0, has_side_effects=True, vmem_limit_bytes=44 * 2 ** 20
            ),
            cost_estimate=pl.CostEstimate(flops=4 * 10 ** 9, bytes_accessed=6 * 10 ** 7, transcendentals=10 ** 6),
        )(*in_hbm(
            positions, freq, hidden, norm_attn.reshape(1, dim), norm_mlp.reshape(1, dim), w_qkv,
            k_cache.reshape(flat), v_cache.reshape(flat), w_out, w_gate_up, w_down,
        ))
        result, k_upd, v_upd, _, _ = pl.pallas_call(
            store_kernel,
            out_shape=(
                jax.ShapeDtypeStruct((rows, dim), BF16),
                jax.ShapeDtypeStruct(flat, BF16),
                jax.ShapeDtypeStruct(flat, BF16),
                pltpu.VMEM(flat, BF16),
                pltpu.VMEM(flat, BF16),
            ),
            in_specs=[smem] + [vmem] * 5,
            out_specs=(hbm, hbm, hbm, vmem, vmem),
            input_output_aliases={4: 3, 5: 4},
            scratch_shapes=[
                pltpu.VMEM((rows, dim), BF16),
                pltpu.SemaphoreType.DMA,
                pltpu.SemaphoreType.DMA,
                pltpu.SemaphoreType.DMA,
            ],
            compiler_params=pltpu.CompilerParams(vmem_limit_bytes=8 * 2 ** 20),
            cost_estimate=pl.CostEstimate(flops=10 ** 8, bytes_accessed=2 * 10 ** 7, transcendentals=0),
        )(pos, x2, k_new, v_new, k_mid, v_mid)
        return result, k_upd.reshape(k_cache.shape), v_upd.reshape(v_cache.shape)

    return jax.shard_map(
        local_step, mesh=mesh,
        in_specs=(P("dp", None), P("dp"), P(None), P(None), P(None, "tp"), P("tp", None), P(None, "tp"), P("tp", None), cache_spec, cache_spec),
        out_specs=(P("dp", None), cache_spec, cache_spec), check_vma=False,
    )
```

time: 56.7 us -> 50.2 us (0.89)
  Pallas kernels: 55.9 us -> 49.5 us
    pallas_call x1, Pallas kernels: 49.1 us -> 43.6 us  [local_step(): pl.pallas_call(layer_kernel, out_shape=(pltpu.VMEM((rows, dim), F32), plt...]
    pallas_call x1, Pallas kernels: 6.78 us -> 5.88 us  [local_step(): pl.pallas_call(store_kernel, out_shape=(jax.ShapeDtypeStruct((rows, dim),...]
where the time goes in v4:
time: 50.2 us; the launch traced here: 50.1 us
  Pallas kernels  49.5 us (99%)
  between operations  0.64 us (1%)
    pallas_call x1, Pallas kernels, local_step(): pl.pallas_call(layer_kernel, out_shape=(pltpu.VMEM((rows, dim), F32), plt...  43.6 us
    pallas_call x1, Pallas kernels, local_step(): pl.pallas_call(store_kernel, out_shape=(jax.ShapeDtypeStruct((rows, dim),...  5.88 us

profile of v4, /device:TPU:0, one launch (start us, length us, event | category | flops | bytes accessed | tf_op | source)
XLA Modules:
  0.0 50.1 jit_solution(18136583778936659561)
XLA Ops:
  0.6 43.6 %shard_map.130 = (f32[16,4096]{1,0:T(8,128)S(1)}, bf16[16,2048,128]{2,1,0:T(8,128)(2,1)S(1)}, bf16[16,2048,128]{2,1,0:T(8,128)(2,1)S(1)}, f32[2,16,128]{2,1,0:T(...) custom-call(s32[16]{0:T(128)} %pos_ref.1, f32[1,128]{1,0:T(1,128)} %constant.2.clone.freq_ref, ...), custom_call_target="tpu_custom_call" | custom-call | flops 4000000000 | bytes 60000000 | tf_op jit(solution)/shard_map/pallas_call | solution.py:398
  44.2 5.9 %shard_map.131 = (bf16[16,4096]{1,0:T(8,128)(2,1)}, bf16[16,2048,128]{2,1,0:T(8,128)(2,1)}, bf16[16,2048,128]{2,1,0:T(8,128)(2,1)}, bf16[16,2048,128]{2,1,0:T(8,128)(2,1)S(1)}, bf16[16,2048,128]{2,1,0:T(8,128)(2,1)S(1)}) custom-call(s32[16]{0:T(128)S(4)} %get-tuple-element.12.pos, ...), custom_call_target="tpu_custom_call", output_to_operand_aliasing={{3}: (4, {}), {4}: (5, {})} | custom-call | flops 100000000 | bytes 20000000 | tf_op jit(solution)/shard_map/pallas_call | solution.py:459

commit v5 on v4

--- a/solution.py
+++ b/solution.py
@@ -16,8 +16,9 @@
 
 TP = 4
 SP = 4
-W_CHUNKS = 8
-GROUP = 4
+W_CHUNKS = 4
+GROUP = 2
+FLIGHT = 3
 OFFSETS = (
     (0, 1), (0, 3), (1, 1), (2, 1), (1, 3), (3, 1), (2, 3), (3, 3),
     (0, 2), (1, 0), (2, 0), (1, 2), (3, 0), (2, 2), (3, 2),
@@ -32,11 +33,11 @@
 def layer_kernel(
     pos_ref, freq_ref, x_ref, gain_ref, gain2_ref, wq_ref, k_ref, v_ref, wo_ref, wg_ref, wd_ref,
     out_ref, k_buf, v_buf, kn_buf, vn_buf, pos,
-    freq, x_buf, gain, gain2, wq_buf, wo_buf, wg_buf, wd_buf,
-    r_buf, q_buf, part, part_rx, o_buf, ob_buf, rs_tx, rs_rx, ag_buf, ss_buf, r2_buf,
+    freq, x_buf, gain, gain2, wo_buf, wg_buf, wd_buf,
+    r_buf, qkv_buf, q_buf, part, part_rx, o_buf, ob_buf, rs_tx, rs_rx, ag_buf, ss_buf,
     act_buf, dn_buf, rs2_tx, rs2_rx, ag2_buf,
     in_sem, wq_sem, k_sem, v_sem, wo_sem, wg_sem, wd_sem,
-    a_sem, b_sem, s_sem, g_sem, c_sem, d_sem, e_sem, send_sem,
+    a_sem, b_sem, s_sem, g_sem, c_sem, d_sem, e_sem, q_sem, send_sem,
 ):
     dp, t, s = lax.axis_index("dp"), lax.axis_index("tp"), lax.axis_index("sp")
     rows, dim = x_ref.shape
@@ -44,6 +45,9 @@
     units = wg_buf.shape[1] // 2
     ffn = wd_ref.shape[0]
     depth = dim // W_CHUNKS
+    core = s & 1
+    q_cols = wq_ref.shape[1] // 2
+    wq_buf = wg_buf.at[:, pl.ds(0, q_cols)]
 
     def peer(off):
         return (dp, t ^ off[0], s ^ off[1])
@@ -72,7 +76,9 @@
         copy.start()
 
     def wq_copy(c):
-        return pltpu.make_async_copy(wq_ref.at[pl.ds(c * depth, depth)], wq_buf.at[c], wq_sem.at[c])
+        at = pl.ds(c * depth, depth)
+        cols = pl.ds(pl.multiple_of(core * q_cols, 128), q_cols)
+        return pltpu.make_async_copy(wq_ref.at[at, cols], wq_buf.at[at], wq_sem.at[c])
 
     def k_copy(g):
         at = pl.ds(g * GROUP, GROUP)
@@ -89,7 +95,7 @@
 
     def start_wg(c):
         for half in range(2):
-            col = pl.multiple_of(half * ffn + s * units, 128)
+            col = pl.multiple_of(half * ffn + core * units, 128)
             pltpu.make_async_copy(
                 wg_ref.at[pl.ds(c * 1024, 1024), pl.ds(col, units)],
                 wg_buf.at[pl.ds(c * 1024, 1024), pl.ds(half * units, units)],
@@ -97,22 +103,33 @@
             ).start()
 
     def start_wd():
-        for c in range(SP):
+        for c in range(2):
             col = pl.multiple_of(s * 1024, 1024)
             pltpu.make_async_copy(
                 wd_ref.at[pl.ds(c * units, units), pl.ds(col, 1024)], wd_buf.at[c], wd_sem
             ).start()
 
-    wq_copy(0).start()
-    wq_copy(1).start()
+    def kv_loads(g):
+        return [k_copy(g), v_copy(g)]
+
+    loads = [[wq_copy(c)] for c in range(W_CHUNKS)] + [kv_loads(g) for g in range(rows // GROUP)]
+
+    def start_load(i):
+        if i < len(loads):
+            for copy in loads[i]:
+                copy.start()
+
+    for i in range(FLIGHT):
+        start_load(i)
     barrier = pltpu.get_barrier_semaphore()
     for off in OFFSETS:
         pl.semaphore_signal(barrier, inc=1, device_id=peer(off), device_id_type=MESH)
 
+    for c in range(FLIGHT):
+        wq_copy(c).wait()
+        start_load(FLIGHT + c)
     for copy in small:
         copy.wait()
-    for c in range(2, W_CHUNKS):
-        wq_copy(c).start()
     x = x_buf[...].astype(F32)
     scale = lax.rsqrt(jnp.mean(x * x, axis=-1, keepdims=True) + NORM_EPS)
     r_buf[...] = (x * scale * gain[...]).astype(BF16)
@@ -120,35 +137,42 @@
     lane_id = lax.broadcasted_iota(jnp.int32, (rows, 128), 1)
     diag = row_id == lane_id
 
-    qkv = None
-    for c in range(W_CHUNKS):
+    def qkv_term(c):
+        at = pl.ds(c * depth, depth)
+        return jnp.dot(r_buf[:, c * depth:(c + 1) * depth], wq_buf[at, :], preferred_element_type=F32)
+
+    qkv = qkv_term(0)
+    for c in range(1, FLIGHT):
+        qkv = qkv + qkv_term(c)
+    pos_col = jnp.zeros((rows, 128), jnp.int32)
+    for b in range(rows):
+        pos_col = jnp.where(row_id == b, pos[b], pos_col)
+    angle = pos_col.astype(F32) * freq[...]
+    cos = jnp.cos(angle)
+    sin = jnp.sin(angle)
+    sin = jnp.where(lane_id < 64, -sin, sin)
+    for c in range(FLIGHT, W_CHUNKS):
         wq_copy(c).wait()
-        if c >= W_CHUNKS - GROUP:
-            k_copy(c - W_CHUNKS + GROUP).start()
-            v_copy(c - W_CHUNKS + GROUP).start()
-        term = jnp.dot(r_buf[:, c * depth:(c + 1) * depth], wq_buf[c], preferred_element_type=F32)
-        qkv = term if qkv is None else qkv + term
-        if c == 1:
-            pos_col = jnp.zeros((rows, 128), jnp.int32)
-            for b in range(rows):
-                pos_col = jnp.where(row_id == b, pos[b], pos_col)
-            angle = pos_col.astype(F32) * freq[...]
-            cos = jnp.cos(angle)
-            sin = jnp.sin(angle)
-            sin = jnp.where(lane_id < 64, -sin, sin)
-
+        start_load(FLIGHT + c)
+        if c == W_CHUNKS - 1:
+            start_load(FLIGHT + c + 1)
+            start_load(FLIGHT + c + 2)
+        qkv = qkv + qkv_term(c)
+
+    qkv_buf[core] = qkv
+    pl.semaphore_wait(barrier, len(OFFSETS))
+    remote(qkv_buf.at[core], qkv_buf.at[core], 7, q_sem, (0, 1)).start()
+    wait_bytes(qkv_buf.at[1 - core], q_sem)
     def rotate(vals):
         out = vals * cos + pltpu.roll(vals, 64, 1) * sin
         return out.astype(BF16).astype(F32)
 
     for kv in range(2):
-        base = kv * 768
         for h in range(4):
-            q_buf[:, kv * 4 + h, :] = rotate(qkv[:, base + h * 128:base + (h + 1) * 128])
-        kn_buf[kv] = rotate(qkv[:, base + 512:base + 640])
-        vn_buf[kv] = qkv[:, base + 640:base + 768].astype(BF16).astype(F32)
-
-    pl.semaphore_wait(barrier, len(OFFSETS))
+            q_buf[:, kv * 4 + h, :] = rotate(qkv_buf[kv, :, h * 128:(h + 1) * 128])
+        kn_buf[kv] = rotate(qkv_buf[kv, :, 512:640])
+        vn_buf[kv] = qkv_buf[kv, :, 640:768].astype(BF16).astype(F32)
+
     first_slot = s * (keys // 2)
     lane = lax.broadcasted_iota(jnp.int32, (8, keys), 1)
     head = lax.broadcasted_iota(jnp.int32, (8, keys), 0)
@@ -177,20 +201,27 @@
     m_all = jnp.zeros((8, 128), F32)
     l_all = jnp.zeros((8, 128), F32)
     n_all = jnp.zeros((8, 128), F32)
-    for g in range(rows // GROUP):
-        ids = range(g * GROUP, (g + 1) * GROUP)
+
+    def group_scores(g):
         k_copy(g).wait()
         v_copy(g).wait()
-        scores = []
-        for b in ids:
-            q = q_buf[b]
-            scores.append(lax.dot_general(
-                q.astype(BF16), k_buf[b], (((1,), (1,)), ((), ())), preferred_element_type=F32
-            ))
-            fresh = jnp.sum(q * new_rows(kn_buf, b), axis=-1, keepdims=True) * scale
-            n_all = jnp.where(lane8 == sub8 + b * 8, fresh, n_all)
+        start_load(W_CHUNKS + FLIGHT + 2 + g)
+        return [
+            lax.dot_general(
+                q_buf[b].astype(BF16), k_buf[b], (((1,), (1,)), ((), ())), preferred_element_type=F32
+            )
+            for b in range(g * GROUP, (g + 1) * GROUP)
+        ]
+
+    pending = group_scores(0)
+    for g in range(groups):
+        ids = range(g * GROUP, (g + 1) * GROUP)
+        scores = pending
+        if g + 1 < groups:
+            pending = group_scores(g + 1)
         probs = []
         for b, sc in zip(ids, scores):
+            fresh = jnp.sum(q_buf[b] * new_rows(kn_buf, b), axis=-1, keepdims=True) * scale
             ploc = pos[b] - first_slot
             mask = own & (slot_id < ploc) & (slot_id >= ploc - WINDOW)
             sc = jnp.where(mask, sc * scale, NEG)
@@ -198,6 +229,7 @@
             w = jnp.where(mask, jnp.exp(sc - m), 0.0)
             l = jnp.sum(w, axis=-1, keepdims=True)
             at = lane8 == sub8 + b * 8
+            n_all = jnp.where(at, fresh, n_all)
             m_all = jnp.where(at, m, m_all)
             l_all = jnp.where(at, l, l_all)
             probs.append(w.astype(BF16))
@@ -208,17 +240,13 @@
             part[rows + 1] = l_all
         for k, off in ((2, (0, 3)), (0, (0, 1))):
             a_copy(g, k, off).start()
-        if g == 1:
+        if g == groups - 2:
             start_wo()
-        if g == 2:
-            start_wg(0)
-            start_wg(1)
-        if g == 3:
-            start_wg(2)
-            start_wg(3)
-            start_wd()
-
-    for g in range(rows // GROUP):
+    for c in range(4):
+        start_wg(c)
+    start_wd()
+
+    for g in range(groups):
         a_copy(g, 2, (0, 3)).wait_recv()
         a_forward(g).start()
     wait_bytes(part_rx.at[0], a_sem.at[groups])
@@ -245,9 +273,11 @@
         ob_buf[:, h * 128:(h + 1) * 128] = o_buf[:, h, :].astype(BF16)
 
     def reduce_scatter(make_term, tx, rx, phase, sem):
-        for dt in (3, 2, 1, 0):
-            tx[dt] = make_term(t ^ dt)
-            remote(tx.at[dt], rx.at[dt], phase, sem, (dt, 1)).start()
+        for dts in ((3,), (2, 1, 0)):
+            for dt in dts:
+                tx[dt] = make_term(t ^ dt)
+            for dt in dts:
+                remote(tx.at[dt], rx.at[dt], phase, sem, (dt, 1)).start()
         wait_bytes(rx, sem)
         return rx[0] + rx[1] + rx[2] + rx[3]
 
@@ -288,7 +318,7 @@
         remote(ss_buf.at[me], ss_buf.at[me], 2, s_sem, off).start()
     gather = Gather(ag_buf, g_sem, 3)
     gather.send((0, 0))
-    for off in OFFSETS[:8]:
+    for off in OFFSETS[:3]:
         gather.wait(off)
     wait_bytes(ss_buf.at[pl.ds(0, len(OFFSETS))], s_sem)
     tot = jnp.sum(ss_buf[...], axis=0)
@@ -296,35 +326,31 @@
     rstd = lax.rsqrt(mean_sq + NORM_EPS)
     wait_bytes(wg_buf, wg_sem)
 
-    def gate_up(ds):
-        block = s ^ ds ^ 1
-        for j in range(TP):
-            at = pl.ds(pl.multiple_of((block * TP + j) * 256, 256), 256)
-            r2_buf[ds, :, j * 256:(j + 1) * 256] = (ag_buf[block * TP + j] * rstd * gain2[:, at]).astype(BF16)
-        at = pl.ds(pl.multiple_of(block * 1024, 1024), 1024)
-        return jnp.dot(r2_buf[ds], wg_buf[at, :], preferred_element_type=F32)
-
-    hid = gate_up(1) + gate_up(3)
+    def gate_up(offs):
+        out = None
+        for off in offs:
+            slot = piece_of(off)
+            at = pl.ds(pl.multiple_of(slot * 256, 256), 256)
+            r2 = (ag_buf[slot] * rstd * gain2[:, at]).astype(BF16)
+            term = jnp.dot(r2, wg_buf[at, :], preferred_element_type=F32)
+            out = term if out is None else out + term
+        return out
+
+    hid = gate_up(((0, 0),) + OFFSETS[:3])
+    for off in OFFSETS[3:8]:
+        gather.wait(off)
+    hid = hid + gate_up(OFFSETS[3:8])
     gather.wait_block(0)
-    hid = hid + gate_up(0)
     gather.wait_block(2)
-    hid = hid + gate_up(2)
+    hid = hid + gate_up(OFFSETS[8:])
     gate, up = hid[:, :units], hid[:, units:]
-    act_buf[s] = (gate * jax.nn.sigmoid(gate) * up).astype(BF16).astype(F32)
-
-    def act_send(slot, k, off):
-        remote(act_buf.at[slot], act_buf.at[slot], 4, c_sem.at[k], off).start()
-
-    act_send(s, 2, (0, 3))
-    act_send(s, 0, (0, 1))
+    act_buf[core] = (gate * jax.nn.sigmoid(gate) * up).astype(BF16).astype(F32)
+
+    remote(act_buf.at[core], act_buf.at[core], 4, c_sem, (0, 1)).start()
     wait_bytes(wd_buf, wd_sem)
-    down = jnp.dot(act_buf[s].astype(BF16), wd_buf[s], preferred_element_type=F32)
-    for k in (0, 2, 1):
-        slot = s ^ (k + 1)
-        remote(act_buf.at[slot], act_buf.at[slot], 4, c_sem.at[k], (0, 1)).wait_recv()
-        if k == 2:
-            act_send(slot, 1, (0, 1))
-        down = down + jnp.dot(act_buf[slot].astype(BF16), wd_buf[slot], preferred_element_type=F32)
+    down = jnp.dot(act_buf[core].astype(BF16), wd_buf[core], preferred_element_type=F32)
+    wait_bytes(act_buf.at[1 - core], c_sem)
+    down = down + jnp.dot(act_buf[1 - core].astype(BF16), wd_buf[1 - core], preferred_element_type=F32)
     down = down.astype(BF16).astype(F32)
     for d in range(TP):
         dn_buf[d] = down[:, d * 256:(d + 1) * 256]
@@ -342,8 +368,8 @@
     for i in range(16):
         out_ref[:, i * 256:(i + 1) * 256] = ag2_buf[i]
     sent = (
-        part_rx, rs_tx, ss_buf.at[pl.ds(0, 15)], ag_buf.at[pl.ds(0, 15)], act_buf.at[pl.ds(0, 3)],
-        rs2_tx, ag2_buf.at[pl.ds(0, 15)],
+        part_rx, rs_tx, ss_buf.at[pl.ds(0, 15)], ag_buf.at[pl.ds(0, 15)], act_buf.at[0],
+        rs2_tx, ag2_buf.at[pl.ds(0, 15)], qkv_buf.at[0],
     )
     for phase, ref in enumerate(sent):
         wait_bytes(ref, send_sem.at[phase])
@@ -393,7 +419,7 @@
         flat = (rows, block_len * kv_local, head_dim)
         freq = ROPE_BASE ** (-np.arange(0, head_dim, 2, dtype=np.float64) / head_dim)
         freq = jnp.asarray(np.concatenate([freq, freq])[None].astype(np.float32))
-        units = w_down.shape[0] // SP
+        units = w_down.shape[0] // 2
         fresh = (kv_local, rows, head_dim)
         x2, k_mid, v_mid, k_new, v_new, pos = pl.pallas_call(
             layer_kernel,
@@ -412,11 +438,11 @@
                 pltpu.VMEM((rows, dim), BF16),
                 pltpu.VMEM((1, dim), F32),
                 pltpu.VMEM((1, dim), F32),
-                pltpu.VMEM((W_CHUNKS, dim // W_CHUNKS, w_qkv.shape[1]), BF16),
                 pltpu.VMEM((TP, 1024, 256), BF16),
                 pltpu.VMEM((dim, 2 * units), BF16),
-                pltpu.VMEM((SP, units, 1024), BF16),
+                pltpu.VMEM((2, units, 1024), BF16),
                 pltpu.VMEM((rows, dim), BF16),
+                pltpu.VMEM((2, rows, w_qkv.shape[1] // 2), F32),
                 pltpu.VMEM((rows, 8, 128), F32),
                 pltpu.VMEM((rows + 2, 8, 128), F32),
                 pltpu.VMEM((3, rows + 2, 8, 128), F32),
@@ -426,8 +452,7 @@
                 pltpu.VMEM((TP, rows, 256), F32),
                 pltpu.VMEM((16, rows, 256), F32),
                 pltpu.VMEM((16, 1, 128), F32),
-                pltpu.VMEM((SP, rows, 1024), BF16),
-                pltpu.VMEM((SP, rows, units), F32),
+                pltpu.VMEM((2, rows, units), F32),
                 pltpu.VMEM((TP, rows, 256), F32),
                 pltpu.VMEM((TP, rows, 256), F32),
                 pltpu.VMEM((TP, rows, 256), F32),
@@ -443,10 +468,11 @@
                 pltpu.SemaphoreType.DMA,
                 pltpu.SemaphoreType.DMA,
                 pltpu.SemaphoreType.DMA((10,)),
-                pltpu.SemaphoreType.DMA((3,)),
+                pltpu.SemaphoreType.DMA,
                 pltpu.SemaphoreType.DMA,
                 pltpu.SemaphoreType.DMA((10,)),
-                pltpu.SemaphoreType.DMA((7,)),
+                pltpu.SemaphoreType.DMA,
+                pltpu.SemaphoreType.DMA((8,)),
             ],
             compiler_params=pltpu.CompilerParams(
                 collective_id=0, has_side_effects=True, vmem_limit_bytes=44 * 2 ** 20

time: 50.2 us -> 47.6 us (0.948)
  Pallas kernels: 49.5 us -> 46.8 us
    pallas_call x1, Pallas kernels: 43.6 us -> 40.9 us  [local_step(): pl.pallas_call(layer_kernel, out_shape=(pltpu.VMEM((rows, dim), F32), plt...]
where the time goes in v5:
time: 47.6 us; the launch traced here: 47.4 us
  Pallas kernels  46.8 us (98%)
  between operations  0.64 us (1%)
    pallas_call x1, Pallas kernels, local_step(): pl.pallas_call(layer_kernel, out_shape=(pltpu.VMEM((rows, dim), F32), plt...  40.9 us
    pallas_call x1, Pallas kernels, local_step(): pl.pallas_call(store_kernel, out_shape=(jax.ShapeDtypeStruct((rows, dim),...  5.88 us

profile of v5, /device:TPU:0, one launch (start us, length us, event | category | flops | bytes accessed | tf_op | source)
XLA Modules:
  0.0 47.4 jit_solution(17352034356053214684)
XLA Ops:
  0.6 40.9 %shard_map.130 = (f32[16,4096]{1,0:T(8,128)S(1)}, bf16[16,2048,128]{2,1,0:T(8,128)(2,1)S(1)}, bf16[16,2048,128]{2,1,0:T(8,128)(2,1)S(1)}, f32[2,16,128]{2,1,0:T(...) custom-call(s32[16]{0:T(128)} %pos_ref.1, f32[1,128]{1,0:T(1,128)} %constant.2.clone.freq_ref, ...), custom_call_target="tpu_custom_call" | custom-call | flops 4000000000 | bytes 60000000 | tf_op jit(solution)/shard_map/pallas_call | solution.py:424
  41.6 5.9 %shard_map.131 = (bf16[16,4096]{1,0:T(8,128)(2,1)}, bf16[16,2048,128]{2,1,0:T(8,128)(2,1)}, bf16[16,2048,128]{2,1,0:T(8,128)(2,1)}, bf16[16,2048,128]{2,1,0:T(8,128)(2,1)S(1)}, bf16[16,2048,128]{2,1,0:T(8,128)(2,1)S(1)}) custom-call(s32[16]{0:T(128)S(4)} %get-tuple-element.12.pos, ...), custom_call_target="tpu_custom_call", output_to_operand_aliasing={{3}: (4, {}), {4}: (5, {})} | custom-call | flops 100000000 | bytes 20000000 | tf_op jit(solution)/shard_map/pallas_call | solution.py:485

commit v6 on v5

--- a/solution.py
+++ b/solution.py
@@ -35,8 +35,8 @@
     out_ref, k_buf, v_buf, kn_buf, vn_buf, pos,
     freq, x_buf, gain, gain2, wo_buf, wg_buf, wd_buf,
     r_buf, qkv_buf, q_buf, part, part_rx, o_buf, ob_buf, rs_tx, rs_rx, ag_buf, ss_buf,
-    act_buf, dn_buf, rs2_tx, rs2_rx, ag2_buf,
-    in_sem, wq_sem, k_sem, v_sem, wo_sem, wg_sem, wd_sem,
+    act_a, act_b, dn_buf, rs2_tx, rs2_rx, ag2_buf,
+    in_sem, wq_sem, k_sem, wo_sem, wg_sem, wd_sem,
     a_sem, b_sem, s_sem, g_sem, c_sem, d_sem, e_sem, q_sem, send_sem,
 ):
     dp, t, s = lax.axis_index("dp"), lax.axis_index("tp"), lax.axis_index("sp")
@@ -86,7 +86,7 @@
 
     def v_copy(g):
         at = pl.ds(g * GROUP, GROUP)
-        return pltpu.make_async_copy(v_ref.at[at], v_buf.at[at], v_sem.at[g])
+        return pltpu.make_async_copy(v_ref.at[at], v_buf.at[at], k_sem.at[g])
 
     def start_wo():
         for d in range(TP):
@@ -125,9 +125,8 @@
     for off in OFFSETS:
         pl.semaphore_signal(barrier, inc=1, device_id=peer(off), device_id_type=MESH)
 
-    for c in range(FLIGHT):
-        wq_copy(c).wait()
-        start_load(FLIGHT + c)
+    wq_copy(0).wait()
+    start_load(FLIGHT)
     for copy in small:
         copy.wait()
     x = x_buf[...].astype(F32)
@@ -142,8 +141,6 @@
         return jnp.dot(r_buf[:, c * depth:(c + 1) * depth], wq_buf[at, :], preferred_element_type=F32)
 
     qkv = qkv_term(0)
-    for c in range(1, FLIGHT):
-        qkv = qkv + qkv_term(c)
     pos_col = jnp.zeros((rows, 128), jnp.int32)
     for b in range(rows):
         pos_col = jnp.where(row_id == b, pos[b], pos_col)
@@ -151,7 +148,7 @@
     cos = jnp.cos(angle)
     sin = jnp.sin(angle)
     sin = jnp.where(lane_id < 64, -sin, sin)
-    for c in range(FLIGHT, W_CHUNKS):
+    for c in range(1, W_CHUNKS):
         wq_copy(c).wait()
         start_load(FLIGHT + c)
         if c == W_CHUNKS - 1:
@@ -191,20 +188,15 @@
 
     groups = rows // GROUP
 
-    def a_copy(g, k, off):
-        recv = a_sem.at[g if k == 2 else groups]
-        return remote(part.at[a_rows(g)], part_rx.at[k, a_rows(g)], 0, recv, off)
-
-    def a_forward(g):
-        return remote(part_rx.at[2, a_rows(g)], part_rx.at[1, a_rows(g)], 0, a_sem.at[groups + 1], (0, 1))
+    def a_start(g, k):
+        remote(part.at[a_rows(g)], part_rx.at[k, a_rows(g)], 0, a_sem.at[k], (0, k + 1)).start()
 
     m_all = jnp.zeros((8, 128), F32)
     l_all = jnp.zeros((8, 128), F32)
     n_all = jnp.zeros((8, 128), F32)
 
     def group_scores(g):
-        k_copy(g).wait()
-        v_copy(g).wait()
+        wait_bytes(k_buf.at[pl.ds(0, 2 * GROUP)], k_sem.at[g])
         start_load(W_CHUNKS + FLIGHT + 2 + g)
         return [
             lax.dot_general(
@@ -238,19 +230,16 @@
         if g == rows // GROUP - 1:
             part[rows] = m_all
             part[rows + 1] = l_all
-        for k, off in ((2, (0, 3)), (0, (0, 1))):
-            a_copy(g, k, off).start()
+        for k in (1, 2, 0):
+            a_start(g, k)
         if g == groups - 2:
             start_wo()
     for c in range(4):
         start_wg(c)
     start_wd()
 
-    for g in range(groups):
-        a_copy(g, 2, (0, 3)).wait_recv()
-        a_forward(g).start()
-    wait_bytes(part_rx.at[0], a_sem.at[groups])
-    wait_bytes(part_rx.at[1], a_sem.at[groups + 1])
+    for k in range(3):
+        wait_bytes(part_rx.at[k], a_sem.at[k])
     parts = [part, part_rx.at[0], part_rx.at[1], part_rx.at[2]]
     top = n_all
     for p in parts:
@@ -326,31 +315,45 @@
     rstd = lax.rsqrt(mean_sq + NORM_EPS)
     wait_bytes(wg_buf, wg_sem)
 
-    def gate_up(offs):
+    def normed(off):
+        slot = piece_of(off)
+        at = pl.ds(pl.multiple_of(slot * 256, 256), 256)
+        return (ag_buf[slot] * rstd * gain2[:, at]).astype(BF16), at
+
+    def gate_up(pieces, cols):
         out = None
-        for off in offs:
-            slot = piece_of(off)
-            at = pl.ds(pl.multiple_of(slot * 256, 256), 256)
-            r2 = (ag_buf[slot] * rstd * gain2[:, at]).astype(BF16)
-            term = jnp.dot(r2, wg_buf[at, :], preferred_element_type=F32)
+        for r2, at in pieces:
+            term = jnp.dot(r2, wg_buf[at, cols], preferred_element_type=F32)
             out = term if out is None else out + term
         return out
 
-    hid = gate_up(((0, 0),) + OFFSETS[:3])
+    whole = slice(0, 2 * units)
+    hid = gate_up([normed(off) for off in ((0, 0),) + OFFSETS[:3]], whole)
     for off in OFFSETS[3:8]:
         gather.wait(off)
-    hid = hid + gate_up(OFFSETS[3:8])
+    hid = hid + gate_up([normed(off) for off in OFFSETS[3:8]], whole)
     gather.wait_block(0)
     gather.wait_block(2)
-    hid = hid + gate_up(OFFSETS[8:])
-    gate, up = hid[:, :units], hid[:, units:]
-    act_buf[core] = (gate * jax.nn.sigmoid(gate) * up).astype(BF16).astype(F32)
-
-    remote(act_buf.at[core], act_buf.at[core], 4, c_sem, (0, 1)).start()
+    late = [normed(off) for off in OFFSETS[8:]]
+    acts = (act_a, act_b)
+    spans = (slice(0, act_a.shape[2]), slice(act_a.shape[2], units))
+    for i in range(2):
+        g_cols = spans[i]
+        u_cols = slice(units + g_cols.start, units + g_cols.stop)
+        gate = hid[:, g_cols] + gate_up(late, g_cols)
+        up = hid[:, u_cols] + gate_up(late, u_cols)
+        acts[i][core] = (gate * jax.nn.sigmoid(gate) * up).astype(BF16).astype(F32)
+        remote(acts[i].at[core], acts[i].at[core], 4 + 4 * i, c_sem.at[i], (0, 1)).start()
+
     wait_bytes(wd_buf, wd_sem)
-    down = jnp.dot(act_buf[core].astype(BF16), wd_buf[core], preferred_element_type=F32)
-    wait_bytes(act_buf.at[1 - core], c_sem)
-    down = down + jnp.dot(act_buf[1 - core].astype(BF16), wd_buf[1 - core], preferred_element_type=F32)
+
+    def down_part(i, which):
+        return jnp.dot(acts[i][which].astype(BF16), wd_buf[which, spans[i], :], preferred_element_type=F32)
+
+    down = down_part(0, core) + down_part(1, core)
+    for i in range(2):
+        wait_bytes(acts[i].at[1 - core], c_sem.at[i])
+        down = down + down_part(i, 1 - core)
     down = down.astype(BF16).astype(F32)
     for d in range(TP):
         dn_buf[d] = down[:, d * 256:(d + 1) * 256]
@@ -368,8 +371,8 @@
     for i in range(16):
         out_ref[:, i * 256:(i + 1) * 256] = ag2_buf[i]
     sent = (
-        part_rx, rs_tx, ss_buf.at[pl.ds(0, 15)], ag_buf.at[pl.ds(0, 15)], act_buf.at[0],
-        rs2_tx, ag2_buf.at[pl.ds(0, 15)], qkv_buf.at[0],
+        part_rx, rs_tx, ss_buf.at[pl.ds(0, 15)], ag_buf.at[pl.ds(0, 15)], act_a.at[0],
+        rs2_tx, ag2_buf.at[pl.ds(0, 15)], qkv_buf.at[0], act_b.at[0],
     )
     for phase, ref in enumerate(sent):
         wait_bytes(ref, send_sem.at[phase])
@@ -452,7 +455,8 @@
                 pltpu.VMEM((TP, rows, 256), F32),
                 pltpu.VMEM((16, rows, 256), F32),
                 pltpu.VMEM((16, 1, 128), F32),
-                pltpu.VMEM((2, rows, units), F32),
+                pltpu.VMEM((2, rows, 1024), F32),
+                pltpu.VMEM((2, rows, units - 1024), F32),
                 pltpu.VMEM((TP, rows, 256), F32),
                 pltpu.VMEM((TP, rows, 256), F32),
                 pltpu.VMEM((TP, rows, 256), F32),
@@ -460,19 +464,18 @@
                 pltpu.SemaphoreType.DMA((5,)),
                 pltpu.SemaphoreType.DMA((W_CHUNKS,)),
                 pltpu.SemaphoreType.DMA((rows // GROUP,)),
-                pltpu.SemaphoreType.DMA((rows // GROUP,)),
-                pltpu.SemaphoreType.DMA,
-                pltpu.SemaphoreType.DMA,
-                pltpu.SemaphoreType.DMA,
-                pltpu.SemaphoreType.DMA((rows // GROUP + 2,)),
+                pltpu.SemaphoreType.DMA,
+                pltpu.SemaphoreType.DMA,
+                pltpu.SemaphoreType.DMA,
+                pltpu.SemaphoreType.DMA((3,)),
                 pltpu.SemaphoreType.DMA,
                 pltpu.SemaphoreType.DMA,
                 pltpu.SemaphoreType.DMA((10,)),
-                pltpu.SemaphoreType.DMA,
+                pltpu.SemaphoreType.DMA((2,)),
                 pltpu.SemaphoreType.DMA,
                 pltpu.SemaphoreType.DMA((10,)),
                 pltpu.SemaphoreType.DMA,
-                pltpu.SemaphoreType.DMA((8,)),
+                pltpu.SemaphoreType.DMA((9,)),
             ],
             compiler_params=pltpu.CompilerParams(
                 collective_id=0, has_side_effects=True, vmem_limit_bytes=44 * 2 ** 20

time: 47.6 us -> 45.7 us (0.960)
  Pallas kernels: 46.8 us -> 44.9 us
    pallas_call x1, Pallas kernels: 40.9 us -> 39.1 us  [local_step(): pl.pallas_call(layer_kernel, out_shape=(pltpu.VMEM((rows, dim), F32), plt...]
where the time goes in v6:
time: 45.7 us; the launch traced here: 45.6 us
  Pallas kernels  44.9 us (98%)
  between operations  0.64 us (1%)
    pallas_call x1, Pallas kernels, local_step(): pl.pallas_call(layer_kernel, out_shape=(pltpu.VMEM((rows, dim), F32), plt...  39.1 us
    pallas_call x1, Pallas kernels, local_step(): pl.pallas_call(store_kernel, out_shape=(jax.ShapeDtypeStruct((rows, dim),...  5.88 us

profile of v6, /device:TPU:0, one launch (start us, length us, event | category | flops | bytes accessed | tf_op | source)
XLA Modules:
  0.0 45.6 jit_solution(6853915705953492107)
XLA Ops:
  0.6 39.1 %shard_map.130 = (f32[16,4096]{1,0:T(8,128)S(1)}, bf16[16,2048,128]{2,1,0:T(8,128)(2,1)S(1)}, bf16[16,2048,128]{2,1,0:T(8,128)(2,1)S(1)}, f32[2,16,128]{2,1,0:T(...) custom-call(s32[16]{0:T(128)} %pos_ref.1, f32[1,128]{1,0:T(1,128)} %constant.2.clone.freq_ref, ...), custom_call_target="tpu_custom_call" | custom-call | flops 4000000000 | bytes 60000000 | tf_op jit(solution)/shard_map/pallas_call | solution.py:427
  39.7 5.9 %shard_map.131 = (bf16[16,4096]{1,0:T(8,128)(2,1)}, bf16[16,2048,128]{2,1,0:T(8,128)(2,1)}, bf16[16,2048,128]{2,1,0:T(8,128)(2,1)}, bf16[16,2048,128]{2,1,0:T(8,128)(2,1)S(1)}, bf16[16,2048,128]{2,1,0:T(8,128)(2,1)S(1)}) custom-call(s32[16]{0:T(128)S(4)} %get-tuple-element.12.pos, ...), custom_call_target="tpu_custom_call", output_to_operand_aliasing={{3}: (4, {}), {4}: (5, {})} | custom-call | flops 100000000 | bytes 20000000 | tf_op jit(solution)/shard_map/pallas_call | solution.py:488

commit v7 on v6

--- a/solution.py
+++ b/solution.py
@@ -35,7 +35,7 @@
     out_ref, k_buf, v_buf, kn_buf, vn_buf, pos,
     freq, x_buf, gain, gain2, wo_buf, wg_buf, wd_buf,
     r_buf, qkv_buf, q_buf, part, part_rx, o_buf, ob_buf, rs_tx, rs_rx, ag_buf, ss_buf,
-    act_a, act_b, dn_buf, rs2_tx, rs2_rx, ag2_buf,
+    act_a, act_b, dn_buf, rs2_rx, ag2_buf,
     in_sem, wq_sem, k_sem, wo_sem, wg_sem, wd_sem,
     a_sem, b_sem, s_sem, g_sem, c_sem, d_sem, e_sem, q_sem, send_sem,
 ):
@@ -287,8 +287,8 @@
             self.buf, self.sems, self.phase = buf, sems, phase
 
         def send(self, have):
-            for k in reversed(range(len(OFFSETS))):
-                off = OFFSETS[k]
+            for off in sorted(OFFSETS, key=lambda o: (o[1] != 3 or o[0] == 0, -o[0])):
+                k = OFFSETS.index(off)
                 if add_offsets(off, VIA[off]) == have:
                     slot = piece_of(have)
                     recv = self.sems.at[k if k < 8 else 8 + off[1] // 2]
@@ -358,10 +358,10 @@
     for d in range(TP):
         dn_buf[d] = down[:, d * 256:(d + 1) * 256]
 
-    def down_term(d):
-        return dn_buf[d]
-
-    ag2_buf[me] = mid + reduce_scatter(down_term, rs2_tx, rs2_rx, 5, d_sem)
+    for dt in (3, 2, 1, 0):
+        remote(dn_buf.at[t ^ dt], rs2_rx.at[dt], 5, d_sem, (dt, 1)).start()
+    wait_bytes(rs2_rx, d_sem)
+    ag2_buf[me] = mid + rs2_rx[0] + rs2_rx[1] + rs2_rx[2] + rs2_rx[3]
     gather2 = Gather(ag2_buf, e_sem, 6)
     gather2.send((0, 0))
     for off in OFFSETS[:8]:
@@ -372,7 +372,7 @@
         out_ref[:, i * 256:(i + 1) * 256] = ag2_buf[i]
     sent = (
         part_rx, rs_tx, ss_buf.at[pl.ds(0, 15)], ag_buf.at[pl.ds(0, 15)], act_a.at[0],
-        rs2_tx, ag2_buf.at[pl.ds(0, 15)], qkv_buf.at[0], act_b.at[0],
+        dn_buf, ag2_buf.at[pl.ds(0, 15)], qkv_buf.at[0], act_b.at[0],
     )
     for phase, ref in enumerate(sent):
         wait_bytes(ref, send_sem.at[phase])
@@ -399,9 +399,13 @@
     for b in range(rows):
         ploc = pos[b] - first_slot
         put(k_buf, kn_ref, b, ploc)
-        pltpu.make_async_copy(k_buf.at[b], k_out.at[b], k_sem).start()
+        for h in range(2):
+            at = pl.ds(h * (keys // 2), keys // 2)
+            pltpu.make_async_copy(k_buf.at[b, at], k_out.at[b, at], k_sem).start()
         put(v_buf, vn_ref, b, ploc)
-        pltpu.make_async_copy(v_buf.at[b], v_out.at[b], v_sem).start()
+        for h in range(2):
+            at = pl.ds(h * (keys // 2), keys // 2)
+            pltpu.make_async_copy(v_buf.at[b, at], v_out.at[b, at], v_sem).start()
     out.wait()
     pltpu.make_async_copy(k_buf, k_out, k_sem).wait()
     pltpu.make_async_copy(v_buf, v_out, v_sem).wait()
@@ -459,7 +463,6 @@
                 pltpu.VMEM((2, rows, units - 1024), F32),
                 pltpu.VMEM((TP, rows, 256), F32),
                 pltpu.VMEM((TP, rows, 256), F32),
-                pltpu.VMEM((TP, rows, 256), F32),
                 pltpu.VMEM((16, rows, 256), F32),
                 pltpu.SemaphoreType.DMA((5,)),
                 pltpu.SemaphoreType.DMA((W_CHUNKS,)),

time: 45.7 us -> 45.7 us (level)
  no operation moved by 1% of the time
where the time goes in v7:
time: 45.7 us; the launch traced here: 45.5 us
  Pallas kernels  44.9 us (98%)
  between operations  0.64 us (1%)
    pallas_call x1, Pallas kernels, local_step(): pl.pallas_call(layer_kernel, out_shape=(pltpu.VMEM((rows, dim), F32), plt...  39 us
    pallas_call x1, Pallas kernels, local_step(): pl.pallas_call(store_kernel, out_shape=(jax.ShapeDtypeStruct((rows, dim),...  5.85 us

profile of v7, /device:TPU:0, one launch (start us, length us, event | category | flops | bytes accessed | tf_op | source)
XLA Modules:
  0.0 45.5 jit_solution(12309876914574457306)
XLA Ops:
  0.6 39.0 %shard_map.130 = (f32[16,4096]{1,0:T(8,128)S(1)}, bf16[16,2048,128]{2,1,0:T(8,128)(2,1)S(1)}, bf16[16,2048,128]{2,1,0:T(8,128)(2,1)S(1)}, f32[2,16,128]{2,1,0:T(...) custom-call(s32[16]{0:T(128)} %pos_ref.1, f32[1,128]{1,0:T(1,128)} %constant.2.clone.freq_ref, ...), custom_call_target="tpu_custom_call" | custom-call | flops 4000000000 | bytes 60000000 | tf_op jit(solution)/shard_map/pallas_call | solution.py:431
  39.7 5.9 %shard_map.131 = (bf16[16,4096]{1,0:T(8,128)(2,1)}, bf16[16,2048,128]{2,1,0:T(8,128)(2,1)}, bf16[16,2048,128]{2,1,0:T(8,128)(2,1)}, bf16[16,2048,128]{2,1,0:T(8,128)(2,1)S(1)}, bf16[16,2048,128]{2,1,0:T(8,128)(2,1)S(1)}) custom-call(s32[16]{0:T(128)S(4)} %get-tuple-element.12.pos, ...), custom_call_target="tpu_custom_call", output_to_operand_aliasing={{3}: (4, {}), {4}: (5, {})} | custom-call | flops 100000000 | bytes 20000000 | tf_op jit(solution)/shard_map/pallas_call | solution.py:491
